TPU v7x, 32 devices: a whole 2x2x4 slice. The times are simulated.
32 devices in a mesh: dp: 8 (over z, core), section: 4 (over y, x).
Axes of the slice: x: 2, y: 2, z: 4, core: 2. Of those that a mesh axis runs over, the one named last changes fastest.
Arguments:
- hidden_act: bfloat16 [1024, 14336], P('dp', 'section'), may hold values from -6 to 6
- out_grad: bfloat16 [1024, 4608], P('dp'), may hold values from -0.1875 to 0.1875
- grad_accum: float32 [14336, 4608], P('section', 'dp'), may hold values from -6 to 6
- master_weight: float32 [14336, 4608], P('section', 'dp'), may hold values from -0.046875 to 0.046875
- adam_first: float32 [14336, 4608], P('section', 'dp'), may hold values from -2 to 2
- adam_second: float32 [14336, 4608], P('section', 'dp'), may hold values from 0.1 to 10
- decode_in: bfloat16 [4, 128, 14336], P(None, 'dp', 'section'), may hold values from -6 to 6
- residual_in: bfloat16 [4, 128, 4608], P(None, 'dp'), may hold values from -6 to 6
- norm_gain: bfloat16 [4608], P('section'), may hold values from 0.25 to 1.75
Outputs:
- weight_new: float32 [14336, 4608], P('section', 'dp')
- first_new: float32 [14336, 4608], P('section', 'dp')
- second_new: float32 [14336, 4608], P('section', 'dp')
- decoded: bfloat16 [4, 128, 4608], P(None, 'dp', 'section')
All inputs are finite; a program needn't handle non-finite values.
Results may differ from a plain program's by a relative error of at most 0.0039.
Values may be sent and summed in bfloat16 or wider, within the bound.
No kernel may reach another device: no remote copies, remote signals or barrier semaphores. Data moves between devices by JAX's collectives and lax.ppermute only.
A program may use at most 192 MiB of HBM per device.

v0:
```python
import functools

import jax
import jax.numpy as jnp
from jax import lax
from jax.experimental import pallas as pl
from jax.experimental.pallas import tpu as pltpu
from jax.sharding import PartitionSpec as P


beta_first = 0.9
beta_second = 0.95
learn_rate = 0.002
decay_rate = 0.1
adam_eps = 1e-08
norm_eps = 1e-05
bias_first = 1.0 - 0.9**10
bias_second = 1.0 - 0.95**10


def ring_place(index, length):
    return jnp.where(2 * index < length, 2 * index, 2 * (length - index) - 1)


def ring_index(place, length):
    return jnp.where(place % 2 == 0, place // 2, length - (place + 1) // 2)


def ring_order(length):
    return [2 * i if 2 * i < length else 2 * (length - i) - 1 for i in range(length)]


def ring_pairs(length, cores, step):
    order = ring_order(length)
    return [
        (order[i] * cores + c, order[(i + step) % length] * cores + c)
        for i in range(length)
        for c in range(cores)
    ]


def ring_gather(own, length, cores):
    found = [(0, own)]
    up, down = own, own
    for step in range(1, (length - 1) // 2 + 1):
        up = lax.ppermute(up, "dp", ring_pairs(length, cores, 1))
        down = lax.ppermute(down, "dp", ring_pairs(length, cores, -1))
        found += [(-step, up), (step, down)]
    if length % 2 == 0:
        up = lax.ppermute(up, "dp", ring_pairs(length, cores, 1))
        found += [(length // 2, up)]
    return found


def chip_gather(own, length, cores):
    found = [(0, offset, block) for offset, block in ring_gather(own, length, cores)]
    if cores == 2:
        swap = [(i, i ^ 1) for i in range(length * cores)]
        for _, offset, block in list(found):
            found.append((1, offset, lax.ppermute(block, "dp", swap)))
    return found


def pick_tile(size, most):
    fits = [t for t in range(128, most + 1, 128) if size % t == 0]
    return fits[-1] if fits else size


def pick_spans(hidden, split):
    tile = pick_tile(hidden, 512)
    count = hidden // tile
    small = 2 * count // 7
    if not split or small == 0:
        return tile, [hidden]
    return tile, [(count - 2 * small) * tile, small * tile, small * tile]


def update_body(count, grad_ref, *refs):
    acts, (accum, weight, first, second) = refs[:count], refs[count : count + 4]
    w_out, f_out, s_out, r_out = refs[-4:]
    act = jnp.concatenate([ref[...] for ref in acts], axis=0)
    gradient = jnp.dot(grad_ref[...], act, preferred_element_type=jnp.float32) + accum[...]
    first_new = beta_first * first[...] + (1.0 - beta_first) * gradient
    second_new = beta_second * second[...] + (1.0 - beta_second) * gradient * gradient
    scale = jnp.sqrt(second_new * (1.0 / bias_second)) + adam_eps
    update = first_new * (1.0 / bias_first) / scale
    old = weight[...]
    weight_new = old - learn_rate * (update + decay_rate * old)
    w_out[...] = weight_new
    f_out[...] = first_new
    s_out[...] = second_new
    r_out[...] = weight_new.astype(jnp.bfloat16)


def update_weights(grad_t, acts, state, done, start, tile):
    width, hidden = state[0].shape
    span = acts[0].shape[1]
    skip = start // tile
    block = pl.BlockSpec((width, tile), lambda i: (0, i + skip))
    return pl.pallas_call(
        functools.partial(update_body, len(acts)),
        grid=(span // tile,),
        in_specs=[pl.BlockSpec(grad_t.shape, lambda i: (0, 0))]
        + [pl.BlockSpec((act.shape[0], tile), lambda i: (0, i)) for act in acts]
        + [block] * 4
        + [pl.BlockSpec(memory_space=pl.ANY)] * len(done),
        out_specs=[block] * 4,
        out_shape=[jax.ShapeDtypeStruct((width, hidden), jnp.float32)] * 3
        + [jax.ShapeDtypeStruct((width, hidden), jnp.bfloat16)],
        input_output_aliases={5 + len(acts) + i: i for i in range(len(done))},
        cost_estimate=pl.CostEstimate(
            flops=2 * grad_t.shape[1] * width * span,
            bytes_accessed=30 * width * span,
            transcendentals=2 * width * span,
        ),
        name="update_weights",
    )(grad_t, *acts, *state, *done)


def decode_body(count, rows, places, *refs):
    acts, weight, outs = refs[:count], refs[count], refs[count + 1 : -2]
    total, placed = refs[-2:]
    step = pl.program_id(0)
    act = jnp.concatenate([ref[...] for ref in acts], axis=0)
    term = lax.dot_general(
        act, weight[...], (((1,), (1,)), ((), ())), preferred_element_type=jnp.float32
    )

    @pl.when(step == 0)
    def _():
        total[...] = term

    @pl.when(step > 0)
    def _():
        total[...] += term

    @pl.when(step == pl.num_programs(0) - 1)
    def _():
        for block in range(count):
            placed[places[block]] = total[block * rows : (block + 1) * rows, :]
        each = count // len(outs)
        for i, out in enumerate(outs):
            out[...] = placed[i * each : (i + 1) * each]


def decode_partial(places, acts, weight_t, groups):
    width, hidden = weight_t.shape
    tile = pick_tile(hidden, hidden // 2)
    blocks, rows = len(acts), acts[0].shape[0]
    return pl.pallas_call(
        functools.partial(decode_body, blocks, rows),
        grid_spec=pltpu.PrefetchScalarGridSpec(
            num_scalar_prefetch=1,
            grid=(hidden // tile,),
            in_specs=[pl.BlockSpec((act.shape[0], tile), lambda i, p: (0, i)) for act in acts]
            + [pl.BlockSpec((width, tile), lambda i, p: (0, i))],
            out_specs=[pl.BlockSpec((blocks // groups, rows, width), lambda i, p: (0, 0, 0))] * groups,
            scratch_shapes=[
                pltpu.VMEM((blocks * rows, width), jnp.float32),
                pltpu.VMEM((blocks, rows, width), jnp.float32),
            ],
        ),
        out_shape=[jax.ShapeDtypeStruct((blocks // groups, rows, width), jnp.float32)] * groups,
        cost_estimate=pl.CostEstimate(
            flops=2 * blocks * rows * width * hidden,
            bytes_accessed=2 * hidden * (width + blocks * rows),
            transcendentals=0,
        ),
        name="decode_partial",
    )(places, *acts, weight_t)


def section_sum(value):
    count = lax.axis_size("section")
    if count & (count - 1):
        return lax.psum(value, "section")
    step = 1
    while step < count:
        value = value + lax.ppermute(value, "section", [(i, i ^ step) for i in range(count)])
        step *= 2
    return value


def per_device(
    hidden_act,
    out_grad,
    grad_accum,
    master_weight,
    adam_first,
    adam_second,
    decode_in,
    residual_in,
    norm_gain,
):
    n_dp, n_sec = lax.axis_size("dp"), lax.axis_size("section")
    me, col = lax.axis_index("dp"), lax.axis_index("section")
    cores = 2 if n_dp % 2 == 0 else 1
    length = n_dp // cores
    chip, core = me // cores, me % cores
    spot = ring_index(chip, length)
    tokens, width_all = out_grad.shape
    steps_count, roll_rows, hidden_local = decode_in.shape
    rows = steps_count * roll_rows
    width = width_all // n_dp
    share_width = width_all // n_sec

    tile, spans = pick_spans(hidden_local, length == n_sec)
    pieces = len(spans)
    starts = [sum(spans[:i]) for i in range(pieces)]
    chunks = 2 if length == n_sec else 1
    cut = rows // chunks
    acts, decs = [], []
    for i in range(pieces):
        own = hidden_act[:, starts[i] : starts[i] + spans[i]]
        acts.append(chip_gather(own, length, cores))
    flat_in = decode_in.reshape(rows, hidden_local)
    for i in range(chunks):
        decs.append(chip_gather(flat_in[i * cut : (i + 1) * cut], length, cores))
    sources = jnp.stack(
        [
            ring_place((spot + offset) % length, length) * cores + (core ^ other)
            for other, offset, _ in acts[0]
        ]
    ).astype(jnp.int32)

    part = tokens // n_sec
    offsets = [offset for other, offset, _ in acts[0] if other == 0]
    mine = lax.dynamic_slice_in_dim(out_grad, col * part, part, 0)
    mine = mine.reshape(part, n_dp, width).transpose(1, 0, 2)
    wanted = jnp.stack(
        [
            ring_place((spot - offset) % length, length) * cores + (core ^ other)
            for other in range(cores)
            for offset in offsets
        ]
    )
    mine = mine[wanted].reshape(cores, length, part, width)
    got = [mine[:, 0]]
    for i, offset in enumerate(offsets[1:]):
        got.append(
            lax.ppermute(mine[:, i + 1], "dp", ring_pairs(length, cores, -offset))
        )
    got = jnp.stack(got, axis=1)
    if cores == 2:
        swap = [(i, i ^ 1) for i in range(n_dp)]
        got = jnp.concatenate([got[0], lax.ppermute(got[1], "dp", swap)], axis=0)
    else:
        got = got[0]
    shares = [got]
    for k in range(1, n_sec):
        shares.append(lax.ppermute(got, "section", [(i, (i + k) % n_sec) for i in range(n_sec)]))
    order = (col - jnp.arange(n_sec)) % n_sec
    grads = jnp.stack(shares)[order]
    grads = grads.transpose(1, 0, 2, 3).reshape(n_dp * tokens, width)
    grad_t = grads.T

    state = [x.T for x in (grad_accum, master_weight, adam_first, adam_second)]
    done = []
    for i in range(pieces):
        done = update_weights(grad_t, [block for _, _, block in acts[i]], state, done, starts[i], tile)
    weight_t, first_t, second_t, rounded_t = done

    places = ((sources // cores - col) % n_sec) * cores + ((sources % cores) ^ core)
    streams = []
    for i in range(chunks):
        dec_parts = [block for _, _, block in decs[i]]
        if length == n_sec:
            partial_out = decode_partial(places, dec_parts, rounded_t, n_sec)
            summed = partial_out[0]
            for k in range(1, n_sec):
                summed = summed + lax.ppermute(
                    partial_out[k], "section", [(s, (s + k) % n_sec) for s in range(n_sec)]
                )
            moved = []
            summed = summed.astype(jnp.bfloat16)
            for j in range(cores):
                pairs = [
                    ((a * cores + b) * n_sec + s, (s * cores + (b ^ j)) * n_sec + a)
                    for a in range(length)
                    for b in range(cores)
                    for s in range(n_sec)
                ]
                moved.append(lax.ppermute(summed[j], ("dp", "section"), pairs))
            if cores == 2:
                flip = core == 1
                moved = [
                    jnp.where(flip, moved[1], moved[0]),
                    jnp.where(flip, moved[0], moved[1]),
                ]
            streams.append(jnp.concatenate(moved, axis=1))
        else:
            partial_out = decode_partial(sources, dec_parts, rounded_t, 1)[0]
            back = lax.all_to_all(partial_out, "dp", 0, 0, tiled=True)
            back = back.transpose(1, 0, 2).reshape(rows, width_all)
            streams.append(lax.psum_scatter(back, "section", scatter_dimension=1, tiled=True))

    resid = lax.dynamic_slice_in_dim(
        residual_in.reshape(rows, width_all), col * share_width, share_width, 1
    ).astype(jnp.float32)
    own_stream = resid + jnp.concatenate(streams, axis=0)
    square_sum = section_sum(jnp.sum(own_stream * own_stream, axis=1, keepdims=True))
    mean_square = square_sum / width_all
    normed = own_stream * lax.rsqrt(mean_square + norm_eps) * norm_gain.astype(jnp.float32)
    decoded = normed.astype(jnp.bfloat16).reshape(steps_count, roll_rows, share_width)
    return (weight_t.T, first_t.T, second_t.T, decoded)


def solution(mesh):
    return jax.shard_map(
        per_device,
        mesh=mesh,
        in_specs=(
            P("dp", "section"),
            P("dp", None),
            P("section", "dp"),
            P("section", "dp"),
            P("section", "dp"),
            P("section", "dp"),
            P(None, "dp", "section"),
            P(None, "dp", None),
            P("section"),
        ),
        out_specs=(
            P("section", "dp"),
            P("section", "dp"),
            P("section", "dp"),
            P(None, "dp", "section"),
        ),
        check_vma=False,
    )
```

profile of v0, /device:TPU:0, one launch (start us, length us, event | category | flops | bytes accessed | tf_op | source)
XLA Modules:
  0.0 198.8 jit_solution(14705654179529260521)
XLA Ops:
  0.9 1.0 copy-done
  2.3 0.6 gather_fusion
  2.9 4.1 %collective-permute-start = (bf16[2,32,576]{2,1,0:T(8,128)(2,1)S(1)}, bf16[2,32,576]{2,1,0:T(8,128)(2,1)S(1)}, u32[]{:S(2)}, u32[]{:S(2)}) collective-permute-start(bf16[2,32,576]{2,1,0:T(8,128)(2,1)S(1)} %get-tuple-element.53), channel_id=1, source_target_pairs={{0,16},{4,20},{16,24},{20,28},{24,8},{28,12},{8,0},{12,4},{1,17},{... | collective-permute-start | bytes 221192 | tf_op jit(solution)/shard_map/ppermute | solution.py:241
  7.0 3.0 %collective-permute-start.2 = (bf16[2,32,576]{2,1,0:T(8,128)(2,1)S(1)}, bf16[2,32,576]{2,1,0:T(8,128)(2,1)S(1)}, u32[]{:S(2)}, u32[]{:S(2)}) collective-permute-start(bf16[2,32,576]{2,1,0:T(8,128)(2,1)S(1)} %get-tuple-element.54), channel_id=1, source_target_pairs={{0,24},{4,28},{16,8},{20,12},{24,0},{28,4},{8,16},{12,20},{1,25},{... | collective-permute-start | bytes 221192 | tf_op jit(solution)/shard_map/ppermute | solution.py:241
  10.5 1.7 collective-permute-start.29
  12.2 7.6 %collective-permute-done.1 = bf16[2,32,576]{2,1,0:T(8,128)(2,1)S(1)} collective-permute-done((bf16[2,32,576]{2,1,0:T(8,128)(2,1)S(1)}, bf16[2,32,576]{2,1,0:T(8,128)(2,1)S(1)}, u32[]{:S(2)}, u32[]{:S(2)}) %collective-permute-start.1) | collective-permute-done | bytes 73760 | tf_op jit(solution)/shard_map/ppermute | solution.py:241
  20.1 1.3 collective-permute-done.3
  21.4 3.0 %collective-permute-start.14 = (bf16[128,1024]{1,0:T(8,128)(2,1)S(1)}, bf16[128,1024]{1,0:T(8,128)(2,1)S(1)}, u32[]{:S(2)}, u32[]{:S(2)}) collective-permute-start(bf16[128,1024]{1,0:T(8,128)(2,1)S(1)} %get-tuple-element.44.refs_0_), channel_id=1, source_target_pairs={{0,16},{4,20},{16,24},{20,28},{24,8},{28,12},{8,0},{12,4},{1,17},{... | collective-permute-start | bytes 786440 | tf_op jit(solution)/shard_map/ppermute | solution.py:46
  24.4 12.8 %collective-permute-done.29.refs_2_ = bf16[32,3584]{1,0:T(8,128)(2,1)S(1)} collective-permute-done((bf16[32,3584]{1,0:T(8,128)(2,1)S(1)}, bf16[32,3584]{1,0:T(8,128)(2,1)S(1)}, u32[]{:S(2)}, u32[]{:S(2)}) %collective-permute-start.29) | collective-permute-done | bytes 229408 | tf_op jit(solution)/shard_map/ppermute | solution.py:47
  37.3 2.9 %collective-permute-start.7 = (bf16[128,1024]{1,0:T(8,128)(2,1)S(1)}, bf16[128,1024]{1,0:T(8,128)(2,1)}, u32[]{:S(2)}, u32[]{:S(2)}) collective-permute-start(bf16[128,1024]{1,0:T(8,128)(2,1)S(1)} %get-tuple-element.45.refs_0_), channel_id=1, source_target_pairs={{0,16},{4,20},{16,24},{20,28},{24,8},{28,12},{8,0},{12,4},{1,17},{... | collective-permute-start | bytes 786440 | tf_op jit(solution)/shard_map/ppermute | solution.py:46
  40.2 12.5 %collective-permute-done.41.refs_2_ = bf16[32,3584]{1,0:T(8,128)(2,1)S(1)} collective-permute-done((bf16[32,3584]{1,0:T(8,128)(2,1)S(1)}, bf16[32,3584]{1,0:T(8,128)(2,1)S(1)}, u32[]{:S(2)}, u32[]{:S(2)}) %collective-permute-start.41) | collective-permute-done | bytes 229408 | tf_op jit(solution)/shard_map/ppermute | solution.py:47
  52.8 3.0 %collective-permute-start.21 = (bf16[128,1536]{1,0:T(8,128)(2,1)S(1)}, bf16[128,1536]{1,0:T(8,128)(2,1)}, u32[]{:S(2)}, u32[]{:S(2)}) collective-permute-start(bf16[128,1536]{1,0:T(8,128)(2,1)S(1)} %slice.59.refs_0_), channel_id=1, source_target_pairs={{0,16},{4,20},{16,24},{20,28},{24,8},{28,12},{8,0},{12,4},{1,17},{... | collective-permute-start | bytes 1179656 | tf_op jit(solution)/shard_map/ppermute | solution.py:46
  55.9 0.5 collective-permute-start.10
  56.4 15.0 %collective-permute-done.8.refs_2_ = bf16[128,1024]{1,0:T(8,128)(2,1)S(1)} collective-permute-done((bf16[128,1024]{1,0:T(8,128)(2,1)S(1)}, bf16[128,1024]{1,0:T(8,128)(2,1)S(1)}, u32[]{:S(2)}, u32[]{:S(2)}) %collective-permute-start.8) | collective-permute-done | bytes 262176 | tf_op jit(solution)/shard_map/ppermute | solution.py:47
  71.3 0.7 copy-done.12
  72.1 0.7 copy-done.15
  72.8 1.5 collective-permute-start.4
  74.3 8.8 %collective-permute-done.22.refs_2_ = bf16[128,1536]{1,0:T(8,128)(2,1)} collective-permute-done((bf16[128,1536]{1,0:T(8,128)(2,1)S(1)}, bf16[128,1536]{1,0:T(8,128)(2,1)}, u32[]{:S(2)}, u32[]{:S(2)}) %collective-permute-start.22) | collective-permute-done | bytes 393248 | tf_op jit(solution)/shard_map/ppermute | solution.py:47
  83.3 3.0 %collective-permute-start.23 = (bf16[128,1536]{1,0:T(8,128)(2,1)}, bf16[128,1536]{1,0:T(8,128)(2,1)}, u32[]{:S(2)}, u32[]{:S(2)}) collective-permute-start(bf16[128,1536]{1,0:T(8,128)(2,1)} %collective-permute-done.21.refs_1_), channel_id=1, source_target_pairs={{0,16},{4,20},{16,24},{20,28},{24,8},{28,12},{8,0},{12,4},{1,17},{... | collective-permute-start | bytes 1179656 | tf_op jit(solution)/shard_map/ppermute | solution.py:50
  86.2 1.5 collective-permute-start.5
  87.8 1.4 collective-permute-start.6
  89.2 2.5 %collective-permute-done.42.refs_3_ = bf16[32,3584]{1,0:T(8,128)(2,1)S(1)} collective-permute-done((bf16[32,3584]{1,0:T(8,128)(2,1)S(1)}, bf16[32,3584]{1,0:T(8,128)(2,1)S(1)}, u32[]{:S(2)}, u32[]{:S(2)}) %collective-permute-start.42) | collective-permute-done | bytes 229408 | tf_op jit(solution)/shard_map/ppermute | solution.py:50
  91.7 0.9 collective-permute-start.16
  92.7 3.1 %collective-permute-done.5 = bf16[8,32,576]{2,1,0:T(8,128)(2,1)} collective-permute-done((bf16[8,32,576]{2,1,0:T(8,128)(2,1)S(1)}, bf16[8,32,576]{2,1,0:T(8,128)(2,1)}, u32[]{:S(2)}, u32[]{:S(2)}) %collective-permute-start.5) | collective-permute-done | bytes 294944 | tf_op jit(solution)/shard_map/ppermute | solution.py:251
  95.9 1.2 collective-permute-done.6
  97.5 8.4 %collective-permute-done.16.refs_3_ = bf16[128,1024]{1,0:T(8,128)(2,1)} collective-permute-done((bf16[128,1024]{1,0:T(8,128)(2,1)S(1)}, bf16[128,1024]{1,0:T(8,128)(2,1)}, u32[]{:S(2)}, u32[]{:S(2)}) %collective-permute-start.16) | collective-permute-done | bytes 262176 | tf_op jit(solution)/shard_map/ppermute | solution.py:50
  105.9 0.6 collective-permute-start.26
  106.7 0.5 fusion.2.places
  107.2 0.5 collective-permute-start.11
  107.7 3.2 %collective-permute-done.9.refs_3_ = bf16[128,1024]{1,0:T(8,128)(2,1)S(1)} collective-permute-done((bf16[128,1024]{1,0:T(8,128)(2,1)}, bf16[128,1024]{1,0:T(8,128)(2,1)S(1)}, u32[]{:S(2)}, u32[]{:S(2)}) %collective-permute-start.9) | collective-permute-done | bytes 262176 | tf_op jit(solution)/shard_map/ppermute | solution.py:50
  110.9 0.7 copy-done.16
  111.6 1.3 pad_maximum_fusion
  112.9 0.8 gather_fusion.1
  113.9 1.5 copy.34
  115.4 0.5 collective-permute-start.34
  116.0 14.7 %update_weights.3 = (f32[576,3584]{1,0:T(8,128)}, f32[576,3584]{1,0:T(8,128)}, f32[576,3584]{1,0:T(8,128)}, bf16[576,3584]{1,0:T(8,128)(2,1)}) custom-call(bf16[576,1024]{1,0:T(8,128)(2,1)} %bitcast.89, bf16[128,1536]{1,0:T(8,128)(2,1)} %copy-done.2, bf16[128,1536]{1,0:T(8,128)(2,1)} %collective-permute-done.21.refs_1_, ...), custom_call_target="tpu_custom_call" | custom-call | flops 1811939328 | bytes 26542080 | tf_op jit(solution)/shard_map/update_weights/pallas_call | solution.py:100
  130.7 0.5 collective-permute-start.43
  131.3 9.0 %update_weights.4 = (f32[576,3584]{1,0:T(8,128)}, f32[576,3584]{1,0:T(8,128)}, f32[576,3584]{1,0:T(8,128)}, bf16[576,3584]{1,0:T(8,128)(2,1)}) custom-call(bf16[576,1024]{1,0:T(8,128)(2,1)} %bitcast.90, bf16[128,1024]{1,0:T(8,128)(2,1)} %copy-done.4, ...), custom_call_target="tpu_custom_call", output_to_operand_aliasing={{0}: (13, {}), {1}: (14, {}), {2}: (15, {}), {3}: (16, {})} | custom-call | flops 1207959552 | bytes 17694720 | tf_op jit(solution)/shard_map/update_weights/pallas_call | solution.py:100
  140.3 0.5 collective-permute-start.45
  141.0 0.5 copy-done.21
  141.5 8.9 %update_weights.5 = (f32[576,3584]{1,0:T(8,128)}, f32[576,3584]{1,0:T(8,128)}, f32[576,3584]{1,0:T(8,128)}, bf16[576,3584]{1,0:T(8,128)(2,1)}) custom-call(bf16[576,1024]{1,0:T(8,128)(2,1)} %bitcast.91, bf16[128,1024]{1,0:T(8,128)(2,1)} %copy-done.3, ...), custom_call_target="tpu_custom_call", output_to_operand_aliasing={{0}: (13, {}), {1}: (14, {}), {2}: (15, {}), {3}: (16, {})} | custom-call | flops 1207959552 | bytes 17694720 | tf_op jit(solution)/shard_map/update_weights/pallas_call | solution.py:100
  150.5 0.7 copy-done.37
  151.2 5.6 %decode_partial.2 = (f32[2,32,576]{2,1,0:T(8,128)}, f32[2,32,576]{2,1,0:T(8,128)}, f32[2,32,576]{2,1,0:T(8,128)}, f32[2,32,576]{2,1,0:T(8,128)}) custom-call(s32[8]{0:T(128)} %fusion.2.places, bf16[32,3584]{1,0:T(8,128)(2,1)} %bitcast.103, bf16[32,3584]{1,0:T(8,128)(2,1)} %copy-done.24, bf16[32,3584]{1,0:T(8,128)(2,1)} %copy-done.25, ...), custom_call_target="tpu_custom_call" | custom-call | flops 1056964608 | bytes 5963776 | tf_op jit(solution)/shard_map/decode_partial/pallas_call | solution.py:150
  156.7 2.5 %collective-permute-start.35 = (f32[2,32,576]{2,1,0:T(8,128)}, f32[2,32,576]{2,1,0:T(8,128)S(1)}, u32[]{:S(2)}, u32[]{:S(2)}) collective-permute-start(f32[2,32,576]{2,1,0:T(8,128)} %get-tuple-element.37), channel_id=1, source_target_pairs={{0,1},{1,2},{2,3},{3,0},{4,5},{5,6},{6,7},{7,4},{8,9},{9,10},{10,1... | collective-permute-start | bytes 442376 | tf_op jit(solution)/shard_map/ppermute | solution.py:271
  159.2 1.5 collective-permute-start.36
  160.8 0.4 collective-permute-start.37
  161.5 0.4 copy-done.38
  161.9 0.7 copy-done.39
  162.6 5.6 %decode_partial.3 = (f32[2,32,576]{2,1,0:T(8,128)}, f32[2,32,576]{2,1,0:T(8,128)}, f32[2,32,576]{2,1,0:T(8,128)}, f32[2,32,576]{2,1,0:T(8,128)}) custom-call(s32[8]{0:T(128)} %fusion.2.places, bf16[32,3584]{1,0:T(8,128)(2,1)} %bitcast.98, bf16[32,3584]{1,0:T(8,128)(2,1)} %copy-done.22, bf16[32,3584]{1,0:T(8,128)(2,1)} %copy-done.27, ...), custom_call_target="tpu_custom_call" | custom-call | flops 1056964608 | bytes 5963776 | tf_op jit(solution)/shard_map/decode_partial/pallas_call | solution.py:150
  168.1 1.7 collective-permute-start.47
  169.8 0.5 collective-permute-start.48
  170.3 1.9 collective-permute-start.49
  172.4 0.8 collective-permute-start.39
  173.2 3.1 %collective-permute-done.47 = f32[2,32,576]{2,1,0:T(8,128)S(1)} collective-permute-done((f32[2,32,576]{2,1,0:T(8,128)}, f32[2,32,576]{2,1,0:T(8,128)S(1)}, u32[]{:S(2)}, u32[]{:S(2)}) %collective-permute-start.47) | collective-permute-done | bytes 147488 | tf_op jit(solution)/shard_map/ppermute | solution.py:271
  176.4 1.8 collective-permute-done.48
  178.2 1.0 collective-permute-done.49
  179.1 0.9 add_convert_fusion
  180.2 0.7 collective-permute-start.51
  180.9 0.5 collective-permute-done.50
  181.6 7.3 %collective-permute-start.52 = (f32[64,1]{0,1:T(1,128)S(1)}, f32[64,1]{0,1:T(1,128)S(1)}, u32[]{:S(2)}, u32[]{:S(2)}) collective-permute-start(f32[64,1]{0,1:T(1,128)S(1)} %bitcast.111), channel_id=1, source_target_pairs={{0,1},{1,0},{2,3},{3,2},{4,5},{5,4},{6,7},{7,6},{8,9},{9,8},{10,11... | collective-permute-start | bytes 776 | tf_op jit(solution)/shard_map/ppermute | solution.py:179
  188.9 1.5 collective-permute-done.52
  190.5 6.0 %collective-permute-start.53 = (f32[64,1]{0,1:T(1,128)S(1)}, f32[64,1]{0,1:T(1,128)S(1)}, u32[]{:S(2)}, u32[]{:S(2)}) collective-permute-start(f32[64,1]{0,1:T(1,128)S(1)} %bitcast_add_fusion), channel_id=1, source_target_pairs={{0,2},{1,3},{2,0},{3,1},{4,6},{5,7},{6,4},{7,5},{8,10},{9,11},{10,... | collective-permute-start | bytes 776 | tf_op jit(solution)/shard_map/ppermute | solution.py:179
  196.5 1.5 collective-permute-done.53
  198.1 0.8 multiply_convert_fusion
  (168 shorter events, 3.6 us)
Async XLA Ops:
  2.9 9.3 %collective-permute-start = (bf16[2,32,576]{2,1,0:T(8,128)(2,1)S(1)}, bf16[2,32,576]{2,1,0:T(8,128)(2,1)S(1)}, u32[]{:S(2)}, u32[]{:S(2)}) collective-permute-start(bf16[2,32,576]{2,1,0:T(8,128)(2,1)S(1)} %get-tuple-element.53), channel_id=1, source_target_pairs={{0,16},{4,20},{16,24},{20,28},{24,8},{28,12},{8,0},{12,4},{1,17},{... | collective-permute-start | bytes 221192 | tf_op jit(solution)/shard_map/ppermute | solution.py:241
  7.0 12.8 %collective-permute-start.1 = (bf16[2,32,576]{2,1,0:T(8,128)(2,1)S(1)}, bf16[2,32,576]{2,1,0:T(8,128)(2,1)S(1)}, u32[]{:S(2)}, u32[]{:S(2)}) collective-permute-start(bf16[2,32,576]{2,1,0:T(8,128)(2,1)S(1)} %get-tuple-element.55), channel_id=1, source_target_pairs={{0,8},{4,12},{16,0},{20,4},{24,16},{28,20},{8,24},{12,28},{1,9},{5... | collective-permute-start | bytes 221192 | tf_op jit(solution)/shard_map/ppermute | solution.py:241
  7.0 12.8 %collective-permute-start.2 = (bf16[2,32,576]{2,1,0:T(8,128)(2,1)S(1)}, bf16[2,32,576]{2,1,0:T(8,128)(2,1)S(1)}, u32[]{:S(2)}, u32[]{:S(2)}) collective-permute-start(bf16[2,32,576]{2,1,0:T(8,128)(2,1)S(1)} %get-tuple-element.54), channel_id=1, source_target_pairs={{0,24},{4,28},{16,8},{20,12},{24,0},{28,4},{8,16},{12,20},{1,25},{... | collective-permute-start | bytes 221192 | tf_op jit(solution)/shard_map/ppermute | solution.py:241
  10.1 42.6 %copy-start.6 = (bf16[2,16,3584]{2,1,0:T(8,128)(2,1)}, bf16[2,16,3584]{2,1,0:T(8,128)(2,1)S(1)}, u32[]{:S(2)}) copy-start(bf16[2,16,3584]{2,1,0:T(8,128)(2,1)S(1)} %get-tuple-element.47) | copy-start | bytes 688132
  10.1 42.6 %copy-start.8 = (bf16[2,16,3584]{2,1,0:T(8,128)(2,1)}, bf16[2,16,3584]{2,1,0:T(8,128)(2,1)S(1)}, u32[]{:S(2)}) copy-start(bf16[2,16,3584]{2,1,0:T(8,128)(2,1)S(1)} %get-tuple-element.46) | copy-start | bytes 688132
  10.1 14.2 %collective-permute-start.28 = (bf16[32,3584]{1,0:T(8,128)(2,1)S(1)}, bf16[32,3584]{1,0:T(8,128)(2,1)S(1)}, u32[]{:S(2)}, u32[]{:S(2)}) collective-permute-start(bf16[32,3584]{1,0:T(8,128)(2,1)S(1)} %bitcast.100), channel_id=1, source_target_pairs={{0,16},{4,20},{16,24},{20,28},{24,8},{28,12},{8,0},{12,4},{1,17},{... | collective-permute-start | bytes 688136 | tf_op jit(solution)/shard_map/ppermute | solution.py:46
  10.5 26.6 %collective-permute-start.29 = (bf16[32,3584]{1,0:T(8,128)(2,1)S(1)}, bf16[32,3584]{1,0:T(8,128)(2,1)S(1)}, u32[]{:S(2)}, u32[]{:S(2)}) collective-permute-start(bf16[32,3584]{1,0:T(8,128)(2,1)S(1)} %bitcast.101), channel_id=1, source_target_pairs={{0,8},{4,12},{16,0},{20,4},{24,16},{28,20},{8,24},{12,28},{1,9},{5... | collective-permute-start | bytes 688136 | tf_op jit(solution)/shard_map/ppermute | solution.py:47
  12.2 25.0 %collective-permute-start.31 = (bf16[32,3584]{1,0:T(8,128)(2,1)S(1)}, bf16[32,3584]{1,0:T(8,128)(2,1)S(1)}, u32[]{:S(2)}, u32[]{:S(2)}) collective-permute-start(bf16[32,3584]{1,0:T(8,128)(2,1)S(1)} %bitcast.102), channel_id=1, source_target_pairs={{0,4},{4,0},{8,12},{12,8},{16,20},{20,16},{24,28},{28,24},{1,5},{5... | collective-permute-start | bytes 688136 | tf_op jit(solution)/shard_map/ppermute | solution.py:60
  19.8 17.5 %collective-permute-start.40 = (bf16[32,3584]{1,0:T(8,128)(2,1)S(1)}, bf16[32,3584]{1,0:T(8,128)(2,1)S(1)}, u32[]{:S(2)}, u32[]{:S(2)}) collective-permute-start(bf16[32,3584]{1,0:T(8,128)(2,1)S(1)} %bitcast.96), channel_id=1, source_target_pairs={{0,16},{4,20},{16,24},{20,28},{24,8},{28,12},{8,0},{12,4},{1,17},{... | collective-permute-start | bytes 688136 | tf_op jit(solution)/shard_map/ppermute | solution.py:46
  19.9 1.5 collective-permute-start.3
  20.1 92.8 %copy-start.3 = (bf16[128,1024]{1,0:T(8,128)(2,1)}, bf16[128,1024]{1,0:T(8,128)(2,1)S(1)}, u32[]{:S(2)}) copy-start(bf16[128,1024]{1,0:T(8,128)(2,1)S(1)} %get-tuple-element.45.refs_0_) | copy-start | bytes 786436
  20.1 92.8 %copy-start.4 = (bf16[128,1024]{1,0:T(8,128)(2,1)}, bf16[128,1024]{1,0:T(8,128)(2,1)S(1)}, u32[]{:S(2)}) copy-start(bf16[128,1024]{1,0:T(8,128)(2,1)S(1)} %get-tuple-element.44.refs_0_) | copy-start | bytes 786436
  21.4 31.4 %collective-permute-start.14 = (bf16[128,1024]{1,0:T(8,128)(2,1)S(1)}, bf16[128,1024]{1,0:T(8,128)(2,1)S(1)}, u32[]{:S(2)}, u32[]{:S(2)}) collective-permute-start(bf16[128,1024]{1,0:T(8,128)(2,1)S(1)} %get-tuple-element.44.refs_0_), channel_id=1, source_target_pairs={{0,16},{4,20},{16,24},{20,28},{24,8},{28,12},{8,0},{12,4},{1,17},{... | collective-permute-start | bytes 786440 | tf_op jit(solution)/shard_map/ppermute | solution.py:46
  24.4 82.1 %copy-start.24 = (bf16[32,3584]{1,0:T(8,128)(2,1)}, bf16[32,3584]{1,0:T(8,128)(2,1)S(1)}, u32[]{:S(2)}) copy-start(bf16[32,3584]{1,0:T(8,128)(2,1)S(1)} %collective-permute-done.28.refs_1_) | copy-start | bytes 688132
  24.4 31.4 %collective-permute-start.15 = (bf16[128,1024]{1,0:T(8,128)(2,1)S(1)}, bf16[128,1024]{1,0:T(8,128)(2,1)S(1)}, u32[]{:S(2)}, u32[]{:S(2)}) collective-permute-start(bf16[128,1024]{1,0:T(8,128)(2,1)S(1)} %get-tuple-element.44.refs_0_), channel_id=1, source_target_pairs={{0,8},{4,12},{16,0},{20,4},{24,16},{28,20},{8,24},{12,28},{1,9},{5... | collective-permute-start | bytes 786440 | tf_op jit(solution)/shard_map/ppermute | solution.py:47
  37.2 69.3 %copy-start.25 = (bf16[32,3584]{1,0:T(8,128)(2,1)}, bf16[32,3584]{1,0:T(8,128)(2,1)S(1)}, u32[]{:S(2)}) copy-start(bf16[32,3584]{1,0:T(8,128)(2,1)S(1)} %collective-permute-done.29.refs_2_) | copy-start | bytes 688132
  37.2 15.5 %collective-permute-start.41 = (bf16[32,3584]{1,0:T(8,128)(2,1)S(1)}, bf16[32,3584]{1,0:T(8,128)(2,1)S(1)}, u32[]{:S(2)}, u32[]{:S(2)}) collective-permute-start(bf16[32,3584]{1,0:T(8,128)(2,1)S(1)} %bitcast.97), channel_id=1, source_target_pairs={{0,8},{4,12},{16,0},{20,4},{24,16},{28,20},{8,24},{12,28},{1,9},{5... | collective-permute-start | bytes 688136 | tf_op jit(solution)/shard_map/ppermute | solution.py:47
  37.2 18.6 %collective-permute-start.17 = (bf16[128,1024]{1,0:T(8,128)(2,1)S(1)}, bf16[128,1024]{1,0:T(8,128)(2,1)}, u32[]{:S(2)}, u32[]{:S(2)}) collective-permute-start(bf16[128,1024]{1,0:T(8,128)(2,1)S(1)} %get-tuple-element.44.refs_0_), channel_id=1, source_target_pairs={{0,4},{4,0},{8,12},{12,8},{16,20},{20,16},{24,28},{28,24},{1,5},{5... | collective-permute-start | bytes 786440 | tf_op jit(solution)/shard_map/ppermute | solution.py:60
  37.3 68.6 %copy-start.22 = (bf16[32,3584]{1,0:T(8,128)(2,1)}, bf16[32,3584]{1,0:T(8,128)(2,1)S(1)}, u32[]{:S(2)}) copy-start(bf16[32,3584]{1,0:T(8,128)(2,1)S(1)} %collective-permute-done.40.refs_1_) | copy-start | bytes 688132
  37.3 18.6 %collective-permute-start.7 = (bf16[128,1024]{1,0:T(8,128)(2,1)S(1)}, bf16[128,1024]{1,0:T(8,128)(2,1)}, u32[]{:S(2)}, u32[]{:S(2)}) collective-permute-start(bf16[128,1024]{1,0:T(8,128)(2,1)S(1)} %get-tuple-element.45.refs_0_), channel_id=1, source_target_pairs={{0,16},{4,20},{16,24},{20,28},{24,8},{28,12},{8,0},{12,4},{1,17},{... | collective-permute-start | bytes 786440 | tf_op jit(solution)/shard_map/ppermute | solution.py:46
  52.7 18.6 %collective-permute-start.8 = (bf16[128,1024]{1,0:T(8,128)(2,1)S(1)}, bf16[128,1024]{1,0:T(8,128)(2,1)S(1)}, u32[]{:S(2)}, u32[]{:S(2)}) collective-permute-start(bf16[128,1024]{1,0:T(8,128)(2,1)S(1)} %get-tuple-element.45.refs_0_), channel_id=1, source_target_pairs={{0,8},{4,12},{16,0},{20,4},{24,16},{28,20},{8,24},{12,28},{1,9},{5... | collective-permute-start | bytes 786440 | tf_op jit(solution)/shard_map/ppermute | solution.py:47
  52.7 60.2 %copy-start.2 = (bf16[128,1536]{1,0:T(8,128)(2,1)}, bf16[128,1536]{1,0:T(8,128)(2,1)S(1)}, u32[]{:S(2)}) copy-start(bf16[128,1536]{1,0:T(8,128)(2,1)S(1)} %slice.59.refs_0_) | copy-start | bytes 1179652
  52.8 44.4 %copy-start.11 = (bf16[128,1024]{1,0:T(8,128)(2,1)}, bf16[128,1024]{1,0:T(8,128)(2,1)S(1)}, u32[]{:S(2)}) copy-start(bf16[128,1024]{1,0:T(8,128)(2,1)S(1)} %collective-permute-done.14.refs_1_) | copy-start | bytes 786436
  52.8 21.6 %collective-permute-start.21 = (bf16[128,1536]{1,0:T(8,128)(2,1)S(1)}, bf16[128,1536]{1,0:T(8,128)(2,1)}, u32[]{:S(2)}, u32[]{:S(2)}) collective-permute-start(bf16[128,1536]{1,0:T(8,128)(2,1)S(1)} %slice.59.refs_0_), channel_id=1, source_target_pairs={{0,16},{4,20},{16,24},{20,28},{24,8},{28,12},{8,0},{12,4},{1,17},{... | collective-permute-start | bytes 1179656 | tf_op jit(solution)/shard_map/ppermute | solution.py:46
  55.7 55.1 %copy-start.14 = (bf16[128,1024]{1,0:T(8,128)(2,1)}, bf16[128,1024]{1,0:T(8,128)(2,1)S(1)}, u32[]{:S(2)}) copy-start(bf16[128,1024]{1,0:T(8,128)(2,1)S(1)} %collective-permute-done.15.refs_2_) | copy-start | bytes 786436
  55.7 27.4 %collective-permute-start.22 = (bf16[128,1536]{1,0:T(8,128)(2,1)S(1)}, bf16[128,1536]{1,0:T(8,128)(2,1)}, u32[]{:S(2)}, u32[]{:S(2)}) collective-permute-start(bf16[128,1536]{1,0:T(8,128)(2,1)S(1)} %slice.59.refs_0_), channel_id=1, source_target_pairs={{0,8},{4,12},{16,0},{20,4},{24,16},{28,20},{8,24},{12,28},{1,9},{5... | collective-permute-start | bytes 1179656 | tf_op jit(solution)/shard_map/ppermute | solution.py:47
  55.8 27.4 %collective-permute-start.24 = (bf16[128,1536]{1,0:T(8,128)(2,1)S(1)}, bf16[128,1536]{1,0:T(8,128)(2,1)S(1)}, u32[]{:S(2)}, u32[]{:S(2)}) collective-permute-start(bf16[128,1536]{1,0:T(8,128)(2,1)S(1)} %slice.59.refs_0_), channel_id=1, source_target_pairs={{0,4},{4,0},{8,12},{12,8},{16,20},{20,16},{24,28},{28,24},{1,5},{5... | collective-permute-start | bytes 1179656 | tf_op jit(solution)/shard_map/ppermute | solution.py:60
  55.9 16.3 %collective-permute-start.10 = (bf16[128,1024]{1,0:T(8,128)(2,1)S(1)}, bf16[128,1024]{1,0:T(8,128)(2,1)S(1)}, u32[]{:S(2)}, u32[]{:S(2)}) collective-permute-start(bf16[128,1024]{1,0:T(8,128)(2,1)S(1)} %get-tuple-element.45.refs_0_), channel_id=1, source_target_pairs={{0,4},{4,0},{8,12},{12,8},{16,20},{20,16},{24,28},{28,24},{1,5},{5... | collective-permute-start | bytes 786440 | tf_op jit(solution)/shard_map/ppermute | solution.py:60
  71.3 11.9 %collective-permute-start.30 = (bf16[32,3584]{1,0:T(8,128)(2,1)S(1)}, bf16[32,3584]{1,0:T(8,128)(2,1)S(1)}, u32[]{:S(2)}, u32[]{:S(2)}) collective-permute-start(bf16[32,3584]{1,0:T(8,128)(2,1)S(1)} %collective-permute-done.28.refs_1_), channel_id=1, source_target_pairs={{0,16},{4,20},{16,24},{20,28},{24,8},{28,12},{8,0},{12,4},{1,17},{... | collective-permute-start | bytes 688136 | tf_op jit(solution)/shard_map/ppermute | solution.py:50
  72.8 19.8 %collective-permute-start.4 = (bf16[8,32,576]{2,1,0:T(8,128)(2,1)S(1)}, bf16[8,32,576]{2,1,0:T(8,128)(2,1)S(1)}, u32[]{:S(2)}, u32[]{:S(2)}) collective-permute-start(bf16[8,32,576]{2,1,0:T(8,128)(2,1)S(1)} %get-tuple-element.49), channel_id=1, source_target_pairs={{0,1},{1,2},{2,3},{3,0},{4,5},{5,6},{6,7},{7,4},{8,9},{9,10},{10,1... | collective-permute-start | bytes 884744 | tf_op jit(solution)/shard_map/ppermute | solution.py:251
  74.3 11.9 %collective-permute-start.32 = (bf16[32,3584]{1,0:T(8,128)(2,1)S(1)}, bf16[32,3584]{1,0:T(8,128)(2,1)S(1)}, u32[]{:S(2)}, u32[]{:S(2)}) collective-permute-start(bf16[32,3584]{1,0:T(8,128)(2,1)S(1)} %collective-permute-done.28.refs_1_), channel_id=1, source_target_pairs={{0,4},{4,0},{8,12},{12,8},{16,20},{20,16},{24,28},{28,24},{1,5},{5... | collective-permute-start | bytes 688136 | tf_op jit(solution)/shard_map/ppermute | solution.py:60
  83.2 4.6 %collective-permute-start.33 = (bf16[32,3584]{1,0:T(8,128)(2,1)S(1)}, bf16[32,3584]{1,0:T(8,128)(2,1)S(1)}, u32[]{:S(2)}, u32[]{:S(2)}) collective-permute-start(bf16[32,3584]{1,0:T(8,128)(2,1)S(1)} %collective-permute-done.29.refs_2_), channel_id=1, source_target_pairs={{0,4},{4,0},{8,12},{12,8},{16,20},{20,16},{24,28},{28,24},{1,5},{5... | collective-permute-start | bytes 688136 | tf_op jit(solution)/shard_map/ppermute | solution.py:60
  83.2 8.5 %collective-permute-start.42 = (bf16[32,3584]{1,0:T(8,128)(2,1)S(1)}, bf16[32,3584]{1,0:T(8,128)(2,1)S(1)}, u32[]{:S(2)}, u32[]{:S(2)}) collective-permute-start(bf16[32,3584]{1,0:T(8,128)(2,1)S(1)} %collective-permute-done.40.refs_1_), channel_id=1, source_target_pairs={{0,16},{4,20},{16,24},{20,28},{24,8},{28,12},{8,0},{12,4},{1,17},{... | collective-permute-start | bytes 688136 | tf_op jit(solution)/shard_map/ppermute | solution.py:50
  83.3 23.2 %collective-permute-start.23 = (bf16[128,1536]{1,0:T(8,128)(2,1)}, bf16[128,1536]{1,0:T(8,128)(2,1)}, u32[]{:S(2)}, u32[]{:S(2)}) collective-permute-start(bf16[128,1536]{1,0:T(8,128)(2,1)} %collective-permute-done.21.refs_1_), channel_id=1, source_target_pairs={{0,16},{4,20},{16,24},{20,28},{24,8},{28,12},{8,0},{12,4},{1,17},{... | collective-permute-start | bytes 1179656 | tf_op jit(solution)/shard_map/ppermute | solution.py:50
  86.2 9.6 %collective-permute-start.5 = (bf16[8,32,576]{2,1,0:T(8,128)(2,1)S(1)}, bf16[8,32,576]{2,1,0:T(8,128)(2,1)}, u32[]{:S(2)}, u32[]{:S(2)}) collective-permute-start(bf16[8,32,576]{2,1,0:T(8,128)(2,1)S(1)} %get-tuple-element.49), channel_id=1, source_target_pairs={{0,2},{1,3},{2,0},{3,1},{4,6},{5,7},{6,4},{7,5},{8,10},{9,11},{10,... | collective-permute-start | bytes 884744 | tf_op jit(solution)/shard_map/ppermute | solution.py:251
  87.8 9.3 %collective-permute-start.6 = (bf16[8,32,576]{2,1,0:T(8,128)(2,1)S(1)}, bf16[8,32,576]{2,1,0:T(8,128)(2,1)}, u32[]{:S(2)}, u32[]{:S(2)}) collective-permute-start(bf16[8,32,576]{2,1,0:T(8,128)(2,1)S(1)} %get-tuple-element.49), channel_id=1, source_target_pairs={{0,3},{1,0},{2,1},{3,2},{4,7},{5,4},{6,5},{7,6},{8,11},{9,8},{10,9... | collective-permute-start | bytes 884744 | tf_op jit(solution)/shard_map/ppermute | solution.py:251
  91.7 14.1 %collective-permute-start.16 = (bf16[128,1024]{1,0:T(8,128)(2,1)S(1)}, bf16[128,1024]{1,0:T(8,128)(2,1)}, u32[]{:S(2)}, u32[]{:S(2)}) collective-permute-start(bf16[128,1024]{1,0:T(8,128)(2,1)S(1)} %collective-permute-done.14.refs_1_), channel_id=1, source_target_pairs={{0,16},{4,20},{16,24},{20,28},{24,8},{28,12},{8,0},{12,4},{1,17},{... | collective-permute-start | bytes 786440 | tf_op jit(solution)/shard_map/ppermute | solution.py:50
  92.6 13.2 %collective-permute-start.18 = (bf16[128,1024]{1,0:T(8,128)(2,1)S(1)}, bf16[128,1024]{1,0:T(8,128)(2,1)S(1)}, u32[]{:S(2)}, u32[]{:S(2)}) collective-permute-start(bf16[128,1024]{1,0:T(8,128)(2,1)S(1)} %collective-permute-done.14.refs_1_), channel_id=1, source_target_pairs={{0,4},{4,0},{8,12},{12,8},{16,20},{20,16},{24,28},{28,24},{1,5},{5... | collective-permute-start | bytes 786440 | tf_op jit(solution)/shard_map/ppermute | solution.py:60
  95.9 11.3 %collective-permute-start.19 = (bf16[128,1024]{1,0:T(8,128)(2,1)S(1)}, bf16[128,1024]{1,0:T(8,128)(2,1)S(1)}, u32[]{:S(2)}, u32[]{:S(2)}) collective-permute-start(bf16[128,1024]{1,0:T(8,128)(2,1)S(1)} %collective-permute-done.15.refs_2_), channel_id=1, source_target_pairs={{0,4},{4,0},{8,12},{12,8},{16,20},{20,16},{24,28},{28,24},{1,5},{5... | collective-permute-start | bytes 786440 | tf_op jit(solution)/shard_map/ppermute | solution.py:60
  97.1 13.7 %collective-permute-start.9 = (bf16[128,1024]{1,0:T(8,128)(2,1)}, bf16[128,1024]{1,0:T(8,128)(2,1)S(1)}, u32[]{:S(2)}, u32[]{:S(2)}) collective-permute-start(bf16[128,1024]{1,0:T(8,128)(2,1)} %collective-permute-done.7.refs_1_), channel_id=1, source_target_pairs={{0,16},{4,20},{16,24},{20,28},{24,8},{28,12},{8,0},{12,4},{1,17},{... | collective-permute-start | bytes 786440 | tf_op jit(solution)/shard_map/ppermute | solution.py:50
  105.9 9.5 %collective-permute-start.25 = (bf16[128,1536]{1,0:T(8,128)(2,1)}, bf16[128,1536]{1,0:T(8,128)(2,1)}, u32[]{:S(2)}, u32[]{:S(2)}) collective-permute-start(bf16[128,1536]{1,0:T(8,128)(2,1)} %collective-permute-done.21.refs_1_), channel_id=1, source_target_pairs={{0,4},{4,0},{8,12},{12,8},{16,20},{20,16},{24,28},{28,24},{1,5},{5... | collective-permute-start | bytes 1179656 | tf_op jit(solution)/shard_map/ppermute | solution.py:60
  105.9 9.5 %collective-permute-start.26 = (bf16[128,1536]{1,0:T(8,128)(2,1)}, bf16[128,1536]{1,0:T(8,128)(2,1)}, u32[]{:S(2)}, u32[]{:S(2)}) collective-permute-start(bf16[128,1536]{1,0:T(8,128)(2,1)} %collective-permute-done.22.refs_2_), channel_id=1, source_target_pairs={{0,4},{4,0},{8,12},{12,8},{16,20},{20,16},{24,28},{28,24},{1,5},{5... | collective-permute-start | bytes 1179656 | tf_op jit(solution)/shard_map/ppermute | solution.py:60
  106.4 9.5 %collective-permute-start.27 = (bf16[128,1536]{1,0:T(8,128)(2,1)}, bf16[128,1536]{1,0:T(8,128)(2,1)}, u32[]{:S(2)}, u32[]{:S(2)}) collective-permute-start(bf16[128,1536]{1,0:T(8,128)(2,1)} %collective-permute-done.23.refs_3_), channel_id=1, source_target_pairs={{0,4},{4,0},{8,12},{12,8},{16,20},{20,16},{24,28},{28,24},{1,5},{5... | collective-permute-start | bytes 1179656 | tf_op jit(solution)/shard_map/ppermute | solution.py:60
  107.2 23.5 %collective-permute-start.11 = (bf16[128,1024]{1,0:T(8,128)(2,1)}, bf16[128,1024]{1,0:T(8,128)(2,1)}, u32[]{:S(2)}, u32[]{:S(2)}) collective-permute-start(bf16[128,1024]{1,0:T(8,128)(2,1)} %collective-permute-done.7.refs_1_), channel_id=1, source_target_pairs={{0,4},{4,0},{8,12},{12,8},{16,20},{20,16},{24,28},{28,24},{1,5},{5... | collective-permute-start | bytes 786440 | tf_op jit(solution)/shard_map/ppermute | solution.py:60
  110.9 20.3 %collective-permute-start.20 = (bf16[128,1024]{1,0:T(8,128)(2,1)}, bf16[128,1024]{1,0:T(8,128)(2,1)}, u32[]{:S(2)}, u32[]{:S(2)}) collective-permute-start(bf16[128,1024]{1,0:T(8,128)(2,1)} %collective-permute-done.16.refs_3_), channel_id=1, source_target_pairs={{0,4},{4,0},{8,12},{12,8},{16,20},{20,16},{24,28},{28,24},{1,5},{5... | collective-permute-start | bytes 786440 | tf_op jit(solution)/shard_map/ppermute | solution.py:60
  115.4 24.9 %collective-permute-start.12 = (bf16[128,1024]{1,0:T(8,128)(2,1)S(1)}, bf16[128,1024]{1,0:T(8,128)(2,1)S(1)}, u32[]{:S(2)}, u32[]{:S(2)}) collective-permute-start(bf16[128,1024]{1,0:T(8,128)(2,1)S(1)} %copy-done.13), channel_id=1, source_target_pairs={{0,4},{4,0},{8,12},{12,8},{16,20},{20,16},{24,28},{28,24},{1,5},{5... | collective-permute-start | bytes 786440 | tf_op jit(solution)/shard_map/ppermute | solution.py:60
  115.4 35.0 %collective-permute-start.34 = (bf16[32,3584]{1,0:T(8,128)(2,1)S(1)}, bf16[32,3584]{1,0:T(8,128)(2,1)S(1)}, u32[]{:S(2)}, u32[]{:S(2)}) collective-permute-start(bf16[32,3584]{1,0:T(8,128)(2,1)S(1)} %copy-done.32), channel_id=1, source_target_pairs={{0,4},{4,0},{8,12},{12,8},{16,20},{20,16},{24,28},{28,24},{1,5},{5... | collective-permute-start | bytes 688136 | tf_op jit(solution)/shard_map/ppermute | solution.py:60
  115.9 24.9 %collective-permute-start.13 = (bf16[128,1024]{1,0:T(8,128)(2,1)S(1)}, bf16[128,1024]{1,0:T(8,128)(2,1)S(1)}, u32[]{:S(2)}, u32[]{:S(2)}) collective-permute-start(bf16[128,1024]{1,0:T(8,128)(2,1)S(1)} %copy-done.17), channel_id=1, source_target_pairs={{0,4},{4,0},{8,12},{12,8},{16,20},{20,16},{24,28},{28,24},{1,5},{5... | collective-permute-start | bytes 786440 | tf_op jit(solution)/shard_map/ppermute | solution.py:60
  130.7 28.5 %collective-permute-start.43 = (bf16[32,3584]{1,0:T(8,128)(2,1)S(1)}, bf16[32,3584]{1,0:T(8,128)(2,1)S(1)}, u32[]{:S(2)}, u32[]{:S(2)}) collective-permute-start(bf16[32,3584]{1,0:T(8,128)(2,1)S(1)} %bitcast.99), channel_id=1, source_target_pairs={{0,4},{4,0},{8,12},{12,8},{16,20},{20,16},{24,28},{28,24},{1,5},{5... | collective-permute-start | bytes 688136 | tf_op jit(solution)/shard_map/ppermute | solution.py:60
  131.2 29.6 %collective-permute-start.44 = (bf16[32,3584]{1,0:T(8,128)(2,1)S(1)}, bf16[32,3584]{1,0:T(8,128)(2,1)S(1)}, u32[]{:S(2)}, u32[]{:S(2)}) collective-permute-start(bf16[32,3584]{1,0:T(8,128)(2,1)S(1)} %copy-done.23), channel_id=1, source_target_pairs={{0,4},{4,0},{8,12},{12,8},{16,20},{20,16},{24,28},{28,24},{1,5},{5... | collective-permute-start | bytes 688136 | tf_op jit(solution)/shard_map/ppermute | solution.py:60
  140.3 20.9 %collective-permute-start.45 = (bf16[32,3584]{1,0:T(8,128)(2,1)S(1)}, bf16[32,3584]{1,0:T(8,128)(2,1)S(1)}, u32[]{:S(2)}, u32[]{:S(2)}) collective-permute-start(bf16[32,3584]{1,0:T(8,128)(2,1)S(1)} %copy-done.28), channel_id=1, source_target_pairs={{0,4},{4,0},{8,12},{12,8},{16,20},{20,16},{24,28},{28,24},{1,5},{5... | collective-permute-start | bytes 688136 | tf_op jit(solution)/shard_map/ppermute | solution.py:60
  140.8 20.4 %collective-permute-start.46 = (bf16[32,3584]{1,0:T(8,128)(2,1)S(1)}, bf16[32,3584]{1,0:T(8,128)(2,1)S(1)}, u32[]{:S(2)}, u32[]{:S(2)}) collective-permute-start(bf16[32,3584]{1,0:T(8,128)(2,1)S(1)} %copy-done.30), channel_id=1, source_target_pairs={{0,4},{4,0},{8,12},{12,8},{16,20},{20,16},{24,28},{28,24},{1,5},{5... | collective-permute-start | bytes 688136 | tf_op jit(solution)/shard_map/ppermute | solution.py:60
  156.7 13.6 %collective-permute-start.35 = (f32[2,32,576]{2,1,0:T(8,128)}, f32[2,32,576]{2,1,0:T(8,128)S(1)}, u32[]{:S(2)}, u32[]{:S(2)}) collective-permute-start(f32[2,32,576]{2,1,0:T(8,128)} %get-tuple-element.37), channel_id=1, source_target_pairs={{0,1},{1,2},{2,3},{3,0},{4,5},{5,6},{6,7},{7,4},{8,9},{9,10},{10,1... | collective-permute-start | bytes 442376 | tf_op jit(solution)/shard_map/ppermute | solution.py:271
  159.2 13.0 %collective-permute-start.36 = (f32[2,32,576]{2,1,0:T(8,128)}, f32[2,32,576]{2,1,0:T(8,128)S(1)}, u32[]{:S(2)}, u32[]{:S(2)}) collective-permute-start(f32[2,32,576]{2,1,0:T(8,128)} %get-tuple-element.38), channel_id=1, source_target_pairs={{0,2},{1,3},{2,0},{3,1},{4,6},{5,7},{6,4},{7,5},{8,10},{9,11},{10,... | collective-permute-start | bytes 442376 | tf_op jit(solution)/shard_map/ppermute | solution.py:271
  160.8 11.5 %collective-permute-start.37 = (f32[2,32,576]{2,1,0:T(8,128)}, f32[2,32,576]{2,1,0:T(8,128)S(1)}, u32[]{:S(2)}, u32[]{:S(2)}) collective-permute-start(f32[2,32,576]{2,1,0:T(8,128)} %get-tuple-element.39), channel_id=1, source_target_pairs={{0,3},{1,0},{2,1},{3,2},{4,7},{5,4},{6,5},{7,6},{8,11},{9,8},{10,9... | collective-permute-start | bytes 442376 | tf_op jit(solution)/shard_map/ppermute | solution.py:271
  168.1 8.2 %collective-permute-start.47 = (f32[2,32,576]{2,1,0:T(8,128)}, f32[2,32,576]{2,1,0:T(8,128)S(1)}, u32[]{:S(2)}, u32[]{:S(2)}) collective-permute-start(f32[2,32,576]{2,1,0:T(8,128)} %get-tuple-element.41), channel_id=1, source_target_pairs={{0,1},{1,2},{2,3},{3,0},{4,5},{5,6},{6,7},{7,4},{8,9},{9,10},{10,1... | collective-permute-start | bytes 442376 | tf_op jit(solution)/shard_map/ppermute | solution.py:271
  169.8 8.4 %collective-permute-start.48 = (f32[2,32,576]{2,1,0:T(8,128)}, f32[2,32,576]{2,1,0:T(8,128)S(1)}, u32[]{:S(2)}, u32[]{:S(2)}) collective-permute-start(f32[2,32,576]{2,1,0:T(8,128)} %get-tuple-element.42), channel_id=1, source_target_pairs={{0,2},{1,3},{2,0},{3,1},{4,6},{5,7},{6,4},{7,5},{8,10},{9,11},{10,... | collective-permute-start | bytes 442376 | tf_op jit(solution)/shard_map/ppermute | solution.py:271
  170.3 8.8 %collective-permute-start.49 = (f32[2,32,576]{2,1,0:T(8,128)}, f32[2,32,576]{2,1,0:T(8,128)S(1)}, u32[]{:S(2)}, u32[]{:S(2)}) collective-permute-start(f32[2,32,576]{2,1,0:T(8,128)} %get-tuple-element.43), channel_id=1, source_target_pairs={{0,3},{1,0},{2,1},{3,2},{4,7},{5,4},{6,5},{7,6},{8,11},{9,8},{10,9... | collective-permute-start | bytes 442376 | tf_op jit(solution)/shard_map/ppermute | solution.py:271
  172.4 8.5 %collective-permute-start.38 = (bf16[32,576]{1,0:T(8,128)(2,1)S(1)}, bf16[32,576]{1,0:T(8,128)(2,1)S(1)}, u32[]{:S(2)}, u32[]{:S(2)}) collective-permute-start(bf16[32,576]{1,0:T(8,128)(2,1)S(1)} %get-tuple-element.58), channel_id=1, source_target_pairs={{0,4},{1,12},{2,20},{3,28},{4,0},{5,8},{6,16},{7,24},{8,5},{9,13},... | collective-permute-start | bytes 110600 | tf_op jit(solution)/shard_map/ppermute | solution.py:283
  172.4 8.4 %collective-permute-start.39 = (bf16[32,576]{1,0:T(8,128)(2,1)S(1)}, bf16[32,576]{1,0:T(8,128)(2,1)S(1)}, u32[]{:S(2)}, u32[]{:S(2)}) collective-permute-start(bf16[32,576]{1,0:T(8,128)(2,1)S(1)} %get-tuple-element.59), channel_id=1, source_target_pairs={{0,0},{1,8},{2,16},{3,24},{4,4},{5,12},{6,20},{7,28},{8,1},{9,9},{... | collective-permute-start | bytes 110600 | tf_op jit(solution)/shard_map/ppermute | solution.py:283
  180.1 1.3 collective-permute-start.50
  180.2 1.2 collective-permute-start.51
  181.6 8.8 %collective-permute-start.52 = (f32[64,1]{0,1:T(1,128)S(1)}, f32[64,1]{0,1:T(1,128)S(1)}, u32[]{:S(2)}, u32[]{:S(2)}) collective-permute-start(f32[64,1]{0,1:T(1,128)S(1)} %bitcast.111), channel_id=1, source_target_pairs={{0,1},{1,0},{2,3},{3,2},{4,5},{5,4},{6,7},{7,6},{8,9},{9,8},{10,11... | collective-permute-start | bytes 776 | tf_op jit(solution)/shard_map/ppermute | solution.py:179
  190.5 7.6 %collective-permute-start.53 = (f32[64,1]{0,1:T(1,128)S(1)}, f32[64,1]{0,1:T(1,128)S(1)}, u32[]{:S(2)}, u32[]{:S(2)}) collective-permute-start(f32[64,1]{0,1:T(1,128)S(1)} %bitcast_add_fusion), channel_id=1, source_target_pairs={{0,2},{1,3},{2,0},{3,1},{4,6},{5,7},{6,4},{7,5},{8,10},{9,11},{10,... | collective-permute-start | bytes 776 | tf_op jit(solution)/shard_map/ppermute | solution.py:179
  (33 other events, 270.0 us)
where the time goes:
time: 199 us
  waiting for transfers between devices  86 us (43%)
  starting transfers between devices  54 us (27%)
  Pallas kernels  43.7 us (22%)
  local copies, waits for them, and re-layouts  9.56 us (5%)
  other arithmetic  4.02 us (2%)
    ppermute x5, waiting for transfers between devices, ring_gather(): down = lax.ppermute(down, 'dp', ring_pairs(length, cores, -1))  49.1 us
    pallas_call x3, Pallas kernels, update_weights(): pl.pallas_call(functools.partial(update_body, len(acts)), grid=(span // t...  32.6 us
    ppermute x10, waiting for transfers between devices, ring_gather(): up = lax.ppermute(up, 'dp', ring_pairs(length, cores, 1))  14.1 us
    ppermute x10, starting transfers between devices, ring_gather(): up = lax.ppermute(up, 'dp', ring_pairs(length, cores, 1))  13.5 us
    ppermute x2, starting transfers between devices, section_sum(): lax.ppermute(value, 'section', [(i, i ^ step) for i in range(count)])  13.3 us
    pallas_call x2, Pallas kernels, decode_partial(): pl.pallas_call(functools.partial(decode_body, blocks, rows), grid_spec=pl...  11.1 us
    ppermute x6, starting transfers between devices, per_device(): lax.ppermute(partial_out[k], 'section', [(s, (s + k) % n_sec) for s in ra...  8.57 us
    ppermute x3, waiting for transfers between devices, per_device(): lax.ppermute(mine[:, i + 1], 'dp', ring_pairs(length, cores, -offset))  7.59 us
  transfers between devices with their start and end apart: 54, of which 17 were waited for; matrix products, arithmetic and copies ran while one was open for 3% of the time, Pallas kernels for 22%

commit v1 on v0

--- a/solution.py
+++ b/solution.py
@@ -1,4 +1,5 @@
 import functools
+import math
 
 import jax
 import jax.numpy as jnp
@@ -71,8 +72,8 @@
     count = hidden // tile
     small = 2 * count // 7
     if not split or small == 0:
-        return tile, [hidden]
-    return tile, [(count - 2 * small) * tile, small * tile, small * tile]
+        return [hidden]
+    return [(count - 2 * small) * tile, small * tile, small * tile]
 
 
 def update_body(count, grad_ref, *refs):
@@ -92,9 +93,10 @@
     r_out[...] = weight_new.astype(jnp.bfloat16)
 
 
-def update_weights(grad_t, acts, state, done, start, tile):
+def update_weights(grad_t, acts, state, done, start):
     width, hidden = state[0].shape
     span = acts[0].shape[1]
+    tile = pick_tile(math.gcd(start, span), 896)
     skip = start // tile
     block = pl.BlockSpec((width, tile), lambda i: (0, i + skip))
     return pl.pallas_call(
@@ -204,7 +206,7 @@
     width = width_all // n_dp
     share_width = width_all // n_sec
 
-    tile, spans = pick_spans(hidden_local, length == n_sec)
+    spans = pick_spans(hidden_local, length == n_sec)
     pieces = len(spans)
     starts = [sum(spans[:i]) for i in range(pieces)]
     chunks = 2 if length == n_sec else 1
@@ -257,7 +259,7 @@
     state = [x.T for x in (grad_accum, master_weight, adam_first, adam_second)]
     done = []
     for i in range(pieces):
-        done = update_weights(grad_t, [block for _, _, block in acts[i]], state, done, starts[i], tile)
+        done = update_weights(grad_t, [block for _, _, block in acts[i]], state, done, starts[i])
     weight_t, first_t, second_t, rounded_t = done
 
     places = ((sources // cores - col) % n_sec) * cores + ((sources % cores) ^ core)

time: 199 us -> 196 us (0.985)
  Pallas kernels: 43.7 us -> 40.6 us
    pallas_call x3, Pallas kernels: 32.6 us -> 29.4 us  [update_weights(): pl.pallas_call(functools.partial(update_body, len(acts)), grid=(span // t...]
  transfers between devices with their start and end apart: 54 -> 54, of which waited for: 17 -> 17; matrix products, arithmetic and copies ran while one was open for 3% -> 3% of each run, Pallas kernels for 22% -> 21%
where the time goes in v1:
time: 196 us
  waiting for transfers between devices  86 us (44%)
  starting transfers between devices  54 us (28%)
  Pallas kernels  40.6 us (21%)
  local copies, waits for them, and re-layouts  9.56 us (5%)
  other arithmetic  4.02 us (2%)
    ppermute x5, waiting for transfers between devices, ring_gather(): down = lax.ppermute(down, 'dp', ring_pairs(length, cores, -1))  49.1 us
    pallas_call x3, Pallas kernels, update_weights(): pl.pallas_call(functools.partial(update_body, len(acts)), grid=(span // t...  29.4 us
    ppermute x10, waiting for transfers between devices, ring_gather(): up = lax.ppermute(up, 'dp', ring_pairs(length, cores, 1))  14.1 us
    ppermute x10, starting transfers between devices, ring_gather(): up = lax.ppermute(up, 'dp', ring_pairs(length, cores, 1))  13.5 us
    ppermute x2, starting transfers between devices, section_sum(): lax.ppermute(value, 'section', [(i, i ^ step) for i in range(count)])  13.1 us
    pallas_call x2, Pallas kernels, decode_partial(): pl.pallas_call(functools.partial(decode_body, blocks, rows), grid_spec=pl...  11.1 us
    ppermute x6, starting transfers between devices, per_device(): lax.ppermute(partial_out[k], 'section', [(s, (s + k) % n_sec) for s in ra...  8.75 us
    ppermute x3, waiting for transfers between devices, per_device(): lax.ppermute(mine[:, i + 1], 'dp', ring_pairs(length, cores, -offset))  7.59 us
  transfers between devices with their start and end apart: 54, of which 17 were waited for; matrix products, arithmetic and copies ran while one was open for 3% of the time, Pallas kernels for 21%

profile of v1, /device:TPU:0, one launch (start us, length us, event | category | flops | bytes accessed | tf_op | source)
XLA Modules:
  0.0 195.7 jit_solution(2838376834762023188)
XLA Ops:
  0.9 1.0 copy-done
  2.3 0.6 gather_fusion
  2.9 4.1 %collective-permute-start = (bf16[2,32,576]{2,1,0:T(8,128)(2,1)S(1)}, bf16[2,32,576]{2,1,0:T(8,128)(2,1)S(1)}, u32[]{:S(2)}, u32[]{:S(2)}) collective-permute-start(bf16[2,32,576]{2,1,0:T(8,128)(2,1)S(1)} %get-tuple-element.53), channel_id=1, source_target_pairs={{0,16},{4,20},{16,24},{20,28},{24,8},{28,12},{8,0},{12,4},{1,17},{... | collective-permute-start | bytes 221192 | tf_op jit(solution)/shard_map/ppermute | solution.py:243
  7.0 3.0 %collective-permute-start.2 = (bf16[2,32,576]{2,1,0:T(8,128)(2,1)S(1)}, bf16[2,32,576]{2,1,0:T(8,128)(2,1)S(1)}, u32[]{:S(2)}, u32[]{:S(2)}) collective-permute-start(bf16[2,32,576]{2,1,0:T(8,128)(2,1)S(1)} %get-tuple-element.54), channel_id=1, source_target_pairs={{0,24},{4,28},{16,8},{20,12},{24,0},{28,4},{8,16},{12,20},{1,25},{... | collective-permute-start | bytes 221192 | tf_op jit(solution)/shard_map/ppermute | solution.py:243
  10.1 0.4 collective-permute-start.28
  10.5 1.7 collective-permute-start.29
  12.2 7.6 %collective-permute-done.1 = bf16[2,32,576]{2,1,0:T(8,128)(2,1)S(1)} collective-permute-done((bf16[2,32,576]{2,1,0:T(8,128)(2,1)S(1)}, bf16[2,32,576]{2,1,0:T(8,128)(2,1)S(1)}, u32[]{:S(2)}, u32[]{:S(2)}) %collective-permute-start.1) | collective-permute-done | bytes 73760 | tf_op jit(solution)/shard_map/ppermute | solution.py:243
  20.1 1.3 collective-permute-done.3
  21.4 3.0 %collective-permute-start.14 = (bf16[128,1024]{1,0:T(8,128)(2,1)S(1)}, bf16[128,1024]{1,0:T(8,128)(2,1)S(1)}, u32[]{:S(2)}, u32[]{:S(2)}) collective-permute-start(bf16[128,1024]{1,0:T(8,128)(2,1)S(1)} %get-tuple-element.44.refs_0_), channel_id=1, source_target_pairs={{0,16},{4,20},{16,24},{20,28},{24,8},{28,12},{8,0},{12,4},{1,17},{... | collective-permute-start | bytes 786440 | tf_op jit(solution)/shard_map/ppermute | solution.py:47
  24.4 12.8 %collective-permute-done.29.refs_2_ = bf16[32,3584]{1,0:T(8,128)(2,1)S(1)} collective-permute-done((bf16[32,3584]{1,0:T(8,128)(2,1)S(1)}, bf16[32,3584]{1,0:T(8,128)(2,1)S(1)}, u32[]{:S(2)}, u32[]{:S(2)}) %collective-permute-start.29) | collective-permute-done | bytes 229408 | tf_op jit(solution)/shard_map/ppermute | solution.py:48
  37.3 2.9 %collective-permute-start.7 = (bf16[128,1024]{1,0:T(8,128)(2,1)S(1)}, bf16[128,1024]{1,0:T(8,128)(2,1)}, u32[]{:S(2)}, u32[]{:S(2)}) collective-permute-start(bf16[128,1024]{1,0:T(8,128)(2,1)S(1)} %get-tuple-element.45.refs_0_), channel_id=1, source_target_pairs={{0,16},{4,20},{16,24},{20,28},{24,8},{28,12},{8,0},{12,4},{1,17},{... | collective-permute-start | bytes 786440 | tf_op jit(solution)/shard_map/ppermute | solution.py:47
  40.2 12.5 %collective-permute-done.41.refs_2_ = bf16[32,3584]{1,0:T(8,128)(2,1)S(1)} collective-permute-done((bf16[32,3584]{1,0:T(8,128)(2,1)S(1)}, bf16[32,3584]{1,0:T(8,128)(2,1)S(1)}, u32[]{:S(2)}, u32[]{:S(2)}) %collective-permute-start.41) | collective-permute-done | bytes 229408 | tf_op jit(solution)/shard_map/ppermute | solution.py:48
  52.8 3.0 %collective-permute-start.21 = (bf16[128,1536]{1,0:T(8,128)(2,1)S(1)}, bf16[128,1536]{1,0:T(8,128)(2,1)}, u32[]{:S(2)}, u32[]{:S(2)}) collective-permute-start(bf16[128,1536]{1,0:T(8,128)(2,1)S(1)} %slice.59.refs_0_), channel_id=1, source_target_pairs={{0,16},{4,20},{16,24},{20,28},{24,8},{28,12},{8,0},{12,4},{1,17},{... | collective-permute-start | bytes 1179656 | tf_op jit(solution)/shard_map/ppermute | solution.py:47
  55.9 0.5 collective-permute-start.10
  56.4 15.0 %collective-permute-done.8.refs_2_ = bf16[128,1024]{1,0:T(8,128)(2,1)S(1)} collective-permute-done((bf16[128,1024]{1,0:T(8,128)(2,1)S(1)}, bf16[128,1024]{1,0:T(8,128)(2,1)S(1)}, u32[]{:S(2)}, u32[]{:S(2)}) %collective-permute-start.8) | collective-permute-done | bytes 262176 | tf_op jit(solution)/shard_map/ppermute | solution.py:48
  71.3 0.7 copy-done.12
  72.1 0.7 copy-done.15
  72.8 1.5 collective-permute-start.4
  74.3 8.8 %collective-permute-done.22.refs_2_ = bf16[128,1536]{1,0:T(8,128)(2,1)} collective-permute-done((bf16[128,1536]{1,0:T(8,128)(2,1)S(1)}, bf16[128,1536]{1,0:T(8,128)(2,1)}, u32[]{:S(2)}, u32[]{:S(2)}) %collective-permute-start.22) | collective-permute-done | bytes 393248 | tf_op jit(solution)/shard_map/ppermute | solution.py:48
  83.3 3.0 %collective-permute-start.23 = (bf16[128,1536]{1,0:T(8,128)(2,1)}, bf16[128,1536]{1,0:T(8,128)(2,1)}, u32[]{:S(2)}, u32[]{:S(2)}) collective-permute-start(bf16[128,1536]{1,0:T(8,128)(2,1)} %collective-permute-done.21.refs_1_), channel_id=1, source_target_pairs={{0,16},{4,20},{16,24},{20,28},{24,8},{28,12},{8,0},{12,4},{1,17},{... | collective-permute-start | bytes 1179656 | tf_op jit(solution)/shard_map/ppermute | solution.py:51
  86.2 1.5 collective-permute-start.5
  87.8 1.4 collective-permute-start.6
  89.2 2.5 %collective-permute-done.42.refs_3_ = bf16[32,3584]{1,0:T(8,128)(2,1)S(1)} collective-permute-done((bf16[32,3584]{1,0:T(8,128)(2,1)S(1)}, bf16[32,3584]{1,0:T(8,128)(2,1)S(1)}, u32[]{:S(2)}, u32[]{:S(2)}) %collective-permute-start.42) | collective-permute-done | bytes 229408 | tf_op jit(solution)/shard_map/ppermute | solution.py:51
  91.7 0.9 collective-permute-start.16
  92.7 3.1 %collective-permute-done.5 = bf16[8,32,576]{2,1,0:T(8,128)(2,1)} collective-permute-done((bf16[8,32,576]{2,1,0:T(8,128)(2,1)S(1)}, bf16[8,32,576]{2,1,0:T(8,128)(2,1)}, u32[]{:S(2)}, u32[]{:S(2)}) %collective-permute-start.5) | collective-permute-done | bytes 294944 | tf_op jit(solution)/shard_map/ppermute | solution.py:253
  95.9 1.2 collective-permute-done.6
  97.5 8.4 %collective-permute-done.16.refs_3_ = bf16[128,1024]{1,0:T(8,128)(2,1)} collective-permute-done((bf16[128,1024]{1,0:T(8,128)(2,1)S(1)}, bf16[128,1024]{1,0:T(8,128)(2,1)}, u32[]{:S(2)}, u32[]{:S(2)}) %collective-permute-start.16) | collective-permute-done | bytes 262176 | tf_op jit(solution)/shard_map/ppermute | solution.py:51
  105.9 0.6 collective-permute-start.26
  106.7 0.5 fusion.2.places
  107.2 0.5 collective-permute-start.11
  107.7 3.2 %collective-permute-done.9.refs_3_ = bf16[128,1024]{1,0:T(8,128)(2,1)S(1)} collective-permute-done((bf16[128,1024]{1,0:T(8,128)(2,1)}, bf16[128,1024]{1,0:T(8,128)(2,1)S(1)}, u32[]{:S(2)}, u32[]{:S(2)}) %collective-permute-start.9) | collective-permute-done | bytes 262176 | tf_op jit(solution)/shard_map/ppermute | solution.py:51
  110.9 0.7 copy-done.16
  111.6 1.3 pad_maximum_fusion
  112.9 0.8 gather_fusion.1
  113.9 1.5 copy.34
  115.4 0.5 collective-permute-start.34
  116.0 11.5 %update_weights.3 = (f32[576,3584]{1,0:T(8,128)}, f32[576,3584]{1,0:T(8,128)}, f32[576,3584]{1,0:T(8,128)}, bf16[576,3584]{1,0:T(8,128)(2,1)}) custom-call(bf16[576,1024]{1,0:T(8,128)(2,1)} %bitcast.89, bf16[128,1536]{1,0:T(8,128)(2,1)} %copy-done.2, bf16[128,1536]{1,0:T(8,128)(2,1)} %collective-permute-done.21.refs_1_, ...), custom_call_target="tpu_custom_call" | custom-call | flops 1811939328 | bytes 26542080 | tf_op jit(solution)/shard_map/update_weights/pallas_call | solution.py:102
  127.5 0.5 collective-permute-start.43
  128.1 9.0 %update_weights.4 = (f32[576,3584]{1,0:T(8,128)}, f32[576,3584]{1,0:T(8,128)}, f32[576,3584]{1,0:T(8,128)}, bf16[576,3584]{1,0:T(8,128)(2,1)}) custom-call(bf16[576,1024]{1,0:T(8,128)(2,1)} %bitcast.90, bf16[128,1024]{1,0:T(8,128)(2,1)} %copy-done.4, ...), custom_call_target="tpu_custom_call", output_to_operand_aliasing={{0}: (13, {}), {1}: (14, {}), {2}: (15, {}), {3}: (16, {})} | custom-call | flops 1207959552 | bytes 17694720 | tf_op jit(solution)/shard_map/update_weights/pallas_call | solution.py:102
  137.1 0.5 collective-permute-start.45
  137.8 0.5 copy-done.21
  138.3 8.9 %update_weights.5 = (f32[576,3584]{1,0:T(8,128)}, f32[576,3584]{1,0:T(8,128)}, f32[576,3584]{1,0:T(8,128)}, bf16[576,3584]{1,0:T(8,128)(2,1)}) custom-call(bf16[576,1024]{1,0:T(8,128)(2,1)} %bitcast.91, bf16[128,1024]{1,0:T(8,128)(2,1)} %copy-done.3, ...), custom_call_target="tpu_custom_call", output_to_operand_aliasing={{0}: (13, {}), {1}: (14, {}), {2}: (15, {}), {3}: (16, {})} | custom-call | flops 1207959552 | bytes 17694720 | tf_op jit(solution)/shard_map/update_weights/pallas_call | solution.py:102
  147.3 0.7 copy-done.37
  148.0 5.6 %decode_partial.2 = (f32[2,32,576]{2,1,0:T(8,128)}, f32[2,32,576]{2,1,0:T(8,128)}, f32[2,32,576]{2,1,0:T(8,128)}, f32[2,32,576]{2,1,0:T(8,128)}) custom-call(s32[8]{0:T(128)} %fusion.2.places, bf16[32,3584]{1,0:T(8,128)(2,1)} %bitcast.103, bf16[32,3584]{1,0:T(8,128)(2,1)} %copy-done.24, bf16[32,3584]{1,0:T(8,128)(2,1)} %copy-done.25, ...), custom_call_target="tpu_custom_call" | custom-call | flops 1056964608 | bytes 5963776 | tf_op jit(solution)/shard_map/decode_partial/pallas_call | solution.py:152
  153.5 2.7 %collective-permute-start.35 = (f32[2,32,576]{2,1,0:T(8,128)}, f32[2,32,576]{2,1,0:T(8,128)S(1)}, u32[]{:S(2)}, u32[]{:S(2)}) collective-permute-start(f32[2,32,576]{2,1,0:T(8,128)} %get-tuple-element.37), channel_id=1, source_target_pairs={{0,1},{1,2},{2,3},{3,0},{4,5},{5,6},{6,7},{7,4},{8,9},{9,10},{10,1... | collective-permute-start | bytes 442376 | tf_op jit(solution)/shard_map/ppermute | solution.py:273
  156.3 1.5 collective-permute-start.36
  158.0 0.4 copy-done.36
  158.7 0.7 copy-done.39
  159.4 5.6 %decode_partial.3 = (f32[2,32,576]{2,1,0:T(8,128)}, f32[2,32,576]{2,1,0:T(8,128)}, f32[2,32,576]{2,1,0:T(8,128)}, f32[2,32,576]{2,1,0:T(8,128)}) custom-call(s32[8]{0:T(128)} %fusion.2.places, bf16[32,3584]{1,0:T(8,128)(2,1)} %bitcast.98, bf16[32,3584]{1,0:T(8,128)(2,1)} %copy-done.22, bf16[32,3584]{1,0:T(8,128)(2,1)} %copy-done.27, ...), custom_call_target="tpu_custom_call" | custom-call | flops 1056964608 | bytes 5963776 | tf_op jit(solution)/shard_map/decode_partial/pallas_call | solution.py:152
  165.0 1.8 collective-permute-start.47
  166.8 0.5 collective-permute-start.48
  167.3 1.9 collective-permute-start.49
  169.4 0.8 collective-permute-start.39
  170.3 3.0 %collective-permute-done.47 = f32[2,32,576]{2,1,0:T(8,128)S(1)} collective-permute-done((f32[2,32,576]{2,1,0:T(8,128)}, f32[2,32,576]{2,1,0:T(8,128)S(1)}, u32[]{:S(2)}, u32[]{:S(2)}) %collective-permute-start.47) | collective-permute-done | bytes 147488 | tf_op jit(solution)/shard_map/ppermute | solution.py:273
  173.2 1.9 collective-permute-done.48
  175.2 1.0 collective-permute-done.49
  176.2 0.9 add_convert_fusion
  177.2 0.7 collective-permute-start.51
  177.9 0.5 collective-permute-done.50
  178.6 7.3 %collective-permute-start.52 = (f32[64,1]{0,1:T(1,128)S(1)}, f32[64,1]{0,1:T(1,128)S(1)}, u32[]{:S(2)}, u32[]{:S(2)}) collective-permute-start(f32[64,1]{0,1:T(1,128)S(1)} %bitcast.111), channel_id=1, source_target_pairs={{0,1},{1,0},{2,3},{3,2},{4,5},{5,4},{6,7},{7,6},{8,9},{9,8},{10,11... | collective-permute-start | bytes 776 | tf_op jit(solution)/shard_map/ppermute | solution.py:181
  185.9 1.5 collective-permute-done.52
  187.5 5.9 %collective-permute-start.53 = (f32[64,1]{0,1:T(1,128)S(1)}, f32[64,1]{0,1:T(1,128)S(1)}, u32[]{:S(2)}, u32[]{:S(2)}) collective-permute-start(f32[64,1]{0,1:T(1,128)S(1)} %bitcast_add_fusion), channel_id=1, source_target_pairs={{0,2},{1,3},{2,0},{3,1},{4,6},{5,7},{6,4},{7,5},{8,10},{9,11},{10,... | collective-permute-start | bytes 776 | tf_op jit(solution)/shard_map/ppermute | solution.py:181
  193.3 1.5 collective-permute-done.53
  194.9 0.8 multiply_convert_fusion
  (168 shorter events, 3.4 us)
Async XLA Ops:
  2.9 9.3 %collective-permute-start = (bf16[2,32,576]{2,1,0:T(8,128)(2,1)S(1)}, bf16[2,32,576]{2,1,0:T(8,128)(2,1)S(1)}, u32[]{:S(2)}, u32[]{:S(2)}) collective-permute-start(bf16[2,32,576]{2,1,0:T(8,128)(2,1)S(1)} %get-tuple-element.53), channel_id=1, source_target_pairs={{0,16},{4,20},{16,24},{20,28},{24,8},{28,12},{8,0},{12,4},{1,17},{... | collective-permute-start | bytes 221192 | tf_op jit(solution)/shard_map/ppermute | solution.py:243
  7.0 12.8 %collective-permute-start.1 = (bf16[2,32,576]{2,1,0:T(8,128)(2,1)S(1)}, bf16[2,32,576]{2,1,0:T(8,128)(2,1)S(1)}, u32[]{:S(2)}, u32[]{:S(2)}) collective-permute-start(bf16[2,32,576]{2,1,0:T(8,128)(2,1)S(1)} %get-tuple-element.55), channel_id=1, source_target_pairs={{0,8},{4,12},{16,0},{20,4},{24,16},{28,20},{8,24},{12,28},{1,9},{5... | collective-permute-start | bytes 221192 | tf_op jit(solution)/shard_map/ppermute | solution.py:243
  7.0 12.8 %collective-permute-start.2 = (bf16[2,32,576]{2,1,0:T(8,128)(2,1)S(1)}, bf16[2,32,576]{2,1,0:T(8,128)(2,1)S(1)}, u32[]{:S(2)}, u32[]{:S(2)}) collective-permute-start(bf16[2,32,576]{2,1,0:T(8,128)(2,1)S(1)} %get-tuple-element.54), channel_id=1, source_target_pairs={{0,24},{4,28},{16,8},{20,12},{24,0},{28,4},{8,16},{12,20},{1,25},{... | collective-permute-start | bytes 221192 | tf_op jit(solution)/shard_map/ppermute | solution.py:243
  10.1 42.6 %copy-start.6 = (bf16[2,16,3584]{2,1,0:T(8,128)(2,1)}, bf16[2,16,3584]{2,1,0:T(8,128)(2,1)S(1)}, u32[]{:S(2)}) copy-start(bf16[2,16,3584]{2,1,0:T(8,128)(2,1)S(1)} %get-tuple-element.47) | copy-start | bytes 688132
  10.1 42.6 %copy-start.8 = (bf16[2,16,3584]{2,1,0:T(8,128)(2,1)}, bf16[2,16,3584]{2,1,0:T(8,128)(2,1)S(1)}, u32[]{:S(2)}) copy-start(bf16[2,16,3584]{2,1,0:T(8,128)(2,1)S(1)} %get-tuple-element.46) | copy-start | bytes 688132
  10.1 14.2 %collective-permute-start.28 = (bf16[32,3584]{1,0:T(8,128)(2,1)S(1)}, bf16[32,3584]{1,0:T(8,128)(2,1)S(1)}, u32[]{:S(2)}, u32[]{:S(2)}) collective-permute-start(bf16[32,3584]{1,0:T(8,128)(2,1)S(1)} %bitcast.100), channel_id=1, source_target_pairs={{0,16},{4,20},{16,24},{20,28},{24,8},{28,12},{8,0},{12,4},{1,17},{... | collective-permute-start | bytes 688136 | tf_op jit(solution)/shard_map/ppermute | solution.py:47
  10.5 26.6 %collective-permute-start.29 = (bf16[32,3584]{1,0:T(8,128)(2,1)S(1)}, bf16[32,3584]{1,0:T(8,128)(2,1)S(1)}, u32[]{:S(2)}, u32[]{:S(2)}) collective-permute-start(bf16[32,3584]{1,0:T(8,128)(2,1)S(1)} %bitcast.101), channel_id=1, source_target_pairs={{0,8},{4,12},{16,0},{20,4},{24,16},{28,20},{8,24},{12,28},{1,9},{5... | collective-permute-start | bytes 688136 | tf_op jit(solution)/shard_map/ppermute | solution.py:48
  12.2 25.0 %collective-permute-start.31 = (bf16[32,3584]{1,0:T(8,128)(2,1)S(1)}, bf16[32,3584]{1,0:T(8,128)(2,1)S(1)}, u32[]{:S(2)}, u32[]{:S(2)}) collective-permute-start(bf16[32,3584]{1,0:T(8,128)(2,1)S(1)} %bitcast.102), channel_id=1, source_target_pairs={{0,4},{4,0},{8,12},{12,8},{16,20},{20,16},{24,28},{28,24},{1,5},{5... | collective-permute-start | bytes 688136 | tf_op jit(solution)/shard_map/ppermute | solution.py:61
  19.8 17.5 %collective-permute-start.40 = (bf16[32,3584]{1,0:T(8,128)(2,1)S(1)}, bf16[32,3584]{1,0:T(8,128)(2,1)S(1)}, u32[]{:S(2)}, u32[]{:S(2)}) collective-permute-start(bf16[32,3584]{1,0:T(8,128)(2,1)S(1)} %bitcast.96), channel_id=1, source_target_pairs={{0,16},{4,20},{16,24},{20,28},{24,8},{28,12},{8,0},{12,4},{1,17},{... | collective-permute-start | bytes 688136 | tf_op jit(solution)/shard_map/ppermute | solution.py:47
  19.9 1.5 collective-permute-start.3
  20.1 92.8 %copy-start.3 = (bf16[128,1024]{1,0:T(8,128)(2,1)}, bf16[128,1024]{1,0:T(8,128)(2,1)S(1)}, u32[]{:S(2)}) copy-start(bf16[128,1024]{1,0:T(8,128)(2,1)S(1)} %get-tuple-element.45.refs_0_) | copy-start | bytes 786436
  20.1 92.8 %copy-start.4 = (bf16[128,1024]{1,0:T(8,128)(2,1)}, bf16[128,1024]{1,0:T(8,128)(2,1)S(1)}, u32[]{:S(2)}) copy-start(bf16[128,1024]{1,0:T(8,128)(2,1)S(1)} %get-tuple-element.44.refs_0_) | copy-start | bytes 786436
  21.4 31.4 %collective-permute-start.14 = (bf16[128,1024]{1,0:T(8,128)(2,1)S(1)}, bf16[128,1024]{1,0:T(8,128)(2,1)S(1)}, u32[]{:S(2)}, u32[]{:S(2)}) collective-permute-start(bf16[128,1024]{1,0:T(8,128)(2,1)S(1)} %get-tuple-element.44.refs_0_), channel_id=1, source_target_pairs={{0,16},{4,20},{16,24},{20,28},{24,8},{28,12},{8,0},{12,4},{1,17},{... | collective-permute-start | bytes 786440 | tf_op jit(solution)/shard_map/ppermute | solution.py:47
  24.4 82.1 %copy-start.24 = (bf16[32,3584]{1,0:T(8,128)(2,1)}, bf16[32,3584]{1,0:T(8,128)(2,1)S(1)}, u32[]{:S(2)}) copy-start(bf16[32,3584]{1,0:T(8,128)(2,1)S(1)} %collective-permute-done.28.refs_1_) | copy-start | bytes 688132
  24.4 31.4 %collective-permute-start.15 = (bf16[128,1024]{1,0:T(8,128)(2,1)S(1)}, bf16[128,1024]{1,0:T(8,128)(2,1)S(1)}, u32[]{:S(2)}, u32[]{:S(2)}) collective-permute-start(bf16[128,1024]{1,0:T(8,128)(2,1)S(1)} %get-tuple-element.44.refs_0_), channel_id=1, source_target_pairs={{0,8},{4,12},{16,0},{20,4},{24,16},{28,20},{8,24},{12,28},{1,9},{5... | collective-permute-start | bytes 786440 | tf_op jit(solution)/shard_map/ppermute | solution.py:48
  37.2 69.3 %copy-start.25 = (bf16[32,3584]{1,0:T(8,128)(2,1)}, bf16[32,3584]{1,0:T(8,128)(2,1)S(1)}, u32[]{:S(2)}) copy-start(bf16[32,3584]{1,0:T(8,128)(2,1)S(1)} %collective-permute-done.29.refs_2_) | copy-start | bytes 688132
  37.2 15.5 %collective-permute-start.41 = (bf16[32,3584]{1,0:T(8,128)(2,1)S(1)}, bf16[32,3584]{1,0:T(8,128)(2,1)S(1)}, u32[]{:S(2)}, u32[]{:S(2)}) collective-permute-start(bf16[32,3584]{1,0:T(8,128)(2,1)S(1)} %bitcast.97), channel_id=1, source_target_pairs={{0,8},{4,12},{16,0},{20,4},{24,16},{28,20},{8,24},{12,28},{1,9},{5... | collective-permute-start | bytes 688136 | tf_op jit(solution)/shard_map/ppermute | solution.py:48
  37.2 18.6 %collective-permute-start.17 = (bf16[128,1024]{1,0:T(8,128)(2,1)S(1)}, bf16[128,1024]{1,0:T(8,128)(2,1)}, u32[]{:S(2)}, u32[]{:S(2)}) collective-permute-start(bf16[128,1024]{1,0:T(8,128)(2,1)S(1)} %get-tuple-element.44.refs_0_), channel_id=1, source_target_pairs={{0,4},{4,0},{8,12},{12,8},{16,20},{20,16},{24,28},{28,24},{1,5},{5... | collective-permute-start | bytes 786440 | tf_op jit(solution)/shard_map/ppermute | solution.py:61
  37.3 68.6 %copy-start.22 = (bf16[32,3584]{1,0:T(8,128)(2,1)}, bf16[32,3584]{1,0:T(8,128)(2,1)S(1)}, u32[]{:S(2)}) copy-start(bf16[32,3584]{1,0:T(8,128)(2,1)S(1)} %collective-permute-done.40.refs_1_) | copy-start | bytes 688132
  37.3 18.6 %collective-permute-start.7 = (bf16[128,1024]{1,0:T(8,128)(2,1)S(1)}, bf16[128,1024]{1,0:T(8,128)(2,1)}, u32[]{:S(2)}, u32[]{:S(2)}) collective-permute-start(bf16[128,1024]{1,0:T(8,128)(2,1)S(1)} %get-tuple-element.45.refs_0_), channel_id=1, source_target_pairs={{0,16},{4,20},{16,24},{20,28},{24,8},{28,12},{8,0},{12,4},{1,17},{... | collective-permute-start | bytes 786440 | tf_op jit(solution)/shard_map/ppermute | solution.py:47
  52.7 18.6 %collective-permute-start.8 = (bf16[128,1024]{1,0:T(8,128)(2,1)S(1)}, bf16[128,1024]{1,0:T(8,128)(2,1)S(1)}, u32[]{:S(2)}, u32[]{:S(2)}) collective-permute-start(bf16[128,1024]{1,0:T(8,128)(2,1)S(1)} %get-tuple-element.45.refs_0_), channel_id=1, source_target_pairs={{0,8},{4,12},{16,0},{20,4},{24,16},{28,20},{8,24},{12,28},{1,9},{5... | collective-permute-start | bytes 786440 | tf_op jit(solution)/shard_map/ppermute | solution.py:48
  52.7 60.2 %copy-start.2 = (bf16[128,1536]{1,0:T(8,128)(2,1)}, bf16[128,1536]{1,0:T(8,128)(2,1)S(1)}, u32[]{:S(2)}) copy-start(bf16[128,1536]{1,0:T(8,128)(2,1)S(1)} %slice.59.refs_0_) | copy-start | bytes 1179652
  52.8 44.4 %copy-start.11 = (bf16[128,1024]{1,0:T(8,128)(2,1)}, bf16[128,1024]{1,0:T(8,128)(2,1)S(1)}, u32[]{:S(2)}) copy-start(bf16[128,1024]{1,0:T(8,128)(2,1)S(1)} %collective-permute-done.14.refs_1_) | copy-start | bytes 786436
  52.8 21.6 %collective-permute-start.21 = (bf16[128,1536]{1,0:T(8,128)(2,1)S(1)}, bf16[128,1536]{1,0:T(8,128)(2,1)}, u32[]{:S(2)}, u32[]{:S(2)}) collective-permute-start(bf16[128,1536]{1,0:T(8,128)(2,1)S(1)} %slice.59.refs_0_), channel_id=1, source_target_pairs={{0,16},{4,20},{16,24},{20,28},{24,8},{28,12},{8,0},{12,4},{1,17},{... | collective-permute-start | bytes 1179656 | tf_op jit(solution)/shard_map/ppermute | solution.py:47
  55.7 55.1 %copy-start.14 = (bf16[128,1024]{1,0:T(8,128)(2,1)}, bf16[128,1024]{1,0:T(8,128)(2,1)S(1)}, u32[]{:S(2)}) copy-start(bf16[128,1024]{1,0:T(8,128)(2,1)S(1)} %collective-permute-done.15.refs_2_) | copy-start | bytes 786436
  55.7 27.4 %collective-permute-start.22 = (bf16[128,1536]{1,0:T(8,128)(2,1)S(1)}, bf16[128,1536]{1,0:T(8,128)(2,1)}, u32[]{:S(2)}, u32[]{:S(2)}) collective-permute-start(bf16[128,1536]{1,0:T(8,128)(2,1)S(1)} %slice.59.refs_0_), channel_id=1, source_target_pairs={{0,8},{4,12},{16,0},{20,4},{24,16},{28,20},{8,24},{12,28},{1,9},{5... | collective-permute-start | bytes 1179656 | tf_op jit(solution)/shard_map/ppermute | solution.py:48
  55.8 27.4 %collective-permute-start.24 = (bf16[128,1536]{1,0:T(8,128)(2,1)S(1)}, bf16[128,1536]{1,0:T(8,128)(2,1)S(1)}, u32[]{:S(2)}, u32[]{:S(2)}) collective-permute-start(bf16[128,1536]{1,0:T(8,128)(2,1)S(1)} %slice.59.refs_0_), channel_id=1, source_target_pairs={{0,4},{4,0},{8,12},{12,8},{16,20},{20,16},{24,28},{28,24},{1,5},{5... | collective-permute-start | bytes 1179656 | tf_op jit(solution)/shard_map/ppermute | solution.py:61
  55.9 16.3 %collective-permute-start.10 = (bf16[128,1024]{1,0:T(8,128)(2,1)S(1)}, bf16[128,1024]{1,0:T(8,128)(2,1)S(1)}, u32[]{:S(2)}, u32[]{:S(2)}) collective-permute-start(bf16[128,1024]{1,0:T(8,128)(2,1)S(1)} %get-tuple-element.45.refs_0_), channel_id=1, source_target_pairs={{0,4},{4,0},{8,12},{12,8},{16,20},{20,16},{24,28},{28,24},{1,5},{5... | collective-permute-start | bytes 786440 | tf_op jit(solution)/shard_map/ppermute | solution.py:61
  71.3 11.9 %collective-permute-start.30 = (bf16[32,3584]{1,0:T(8,128)(2,1)S(1)}, bf16[32,3584]{1,0:T(8,128)(2,1)S(1)}, u32[]{:S(2)}, u32[]{:S(2)}) collective-permute-start(bf16[32,3584]{1,0:T(8,128)(2,1)S(1)} %collective-permute-done.28.refs_1_), channel_id=1, source_target_pairs={{0,16},{4,20},{16,24},{20,28},{24,8},{28,12},{8,0},{12,4},{1,17},{... | collective-permute-start | bytes 688136 | tf_op jit(solution)/shard_map/ppermute | solution.py:51
  72.8 19.8 %collective-permute-start.4 = (bf16[8,32,576]{2,1,0:T(8,128)(2,1)S(1)}, bf16[8,32,576]{2,1,0:T(8,128)(2,1)S(1)}, u32[]{:S(2)}, u32[]{:S(2)}) collective-permute-start(bf16[8,32,576]{2,1,0:T(8,128)(2,1)S(1)} %get-tuple-element.49), channel_id=1, source_target_pairs={{0,1},{1,2},{2,3},{3,0},{4,5},{5,6},{6,7},{7,4},{8,9},{9,10},{10,1... | collective-permute-start | bytes 884744 | tf_op jit(solution)/shard_map/ppermute | solution.py:253
  74.3 11.9 %collective-permute-start.32 = (bf16[32,3584]{1,0:T(8,128)(2,1)S(1)}, bf16[32,3584]{1,0:T(8,128)(2,1)S(1)}, u32[]{:S(2)}, u32[]{:S(2)}) collective-permute-start(bf16[32,3584]{1,0:T(8,128)(2,1)S(1)} %collective-permute-done.28.refs_1_), channel_id=1, source_target_pairs={{0,4},{4,0},{8,12},{12,8},{16,20},{20,16},{24,28},{28,24},{1,5},{5... | collective-permute-start | bytes 688136 | tf_op jit(solution)/shard_map/ppermute | solution.py:61
  83.2 4.6 %collective-permute-start.33 = (bf16[32,3584]{1,0:T(8,128)(2,1)S(1)}, bf16[32,3584]{1,0:T(8,128)(2,1)S(1)}, u32[]{:S(2)}, u32[]{:S(2)}) collective-permute-start(bf16[32,3584]{1,0:T(8,128)(2,1)S(1)} %collective-permute-done.29.refs_2_), channel_id=1, source_target_pairs={{0,4},{4,0},{8,12},{12,8},{16,20},{20,16},{24,28},{28,24},{1,5},{5... | collective-permute-start | bytes 688136 | tf_op jit(solution)/shard_map/ppermute | solution.py:61
  83.2 8.5 %collective-permute-start.42 = (bf16[32,3584]{1,0:T(8,128)(2,1)S(1)}, bf16[32,3584]{1,0:T(8,128)(2,1)S(1)}, u32[]{:S(2)}, u32[]{:S(2)}) collective-permute-start(bf16[32,3584]{1,0:T(8,128)(2,1)S(1)} %collective-permute-done.40.refs_1_), channel_id=1, source_target_pairs={{0,16},{4,20},{16,24},{20,28},{24,8},{28,12},{8,0},{12,4},{1,17},{... | collective-permute-start | bytes 688136 | tf_op jit(solution)/shard_map/ppermute | solution.py:51
  83.3 23.2 %collective-permute-start.23 = (bf16[128,1536]{1,0:T(8,128)(2,1)}, bf16[128,1536]{1,0:T(8,128)(2,1)}, u32[]{:S(2)}, u32[]{:S(2)}) collective-permute-start(bf16[128,1536]{1,0:T(8,128)(2,1)} %collective-permute-done.21.refs_1_), channel_id=1, source_target_pairs={{0,16},{4,20},{16,24},{20,28},{24,8},{28,12},{8,0},{12,4},{1,17},{... | collective-permute-start | bytes 1179656 | tf_op jit(solution)/shard_map/ppermute | solution.py:51
  86.2 9.6 %collective-permute-start.5 = (bf16[8,32,576]{2,1,0:T(8,128)(2,1)S(1)}, bf16[8,32,576]{2,1,0:T(8,128)(2,1)}, u32[]{:S(2)}, u32[]{:S(2)}) collective-permute-start(bf16[8,32,576]{2,1,0:T(8,128)(2,1)S(1)} %get-tuple-element.49), channel_id=1, source_target_pairs={{0,2},{1,3},{2,0},{3,1},{4,6},{5,7},{6,4},{7,5},{8,10},{9,11},{10,... | collective-permute-start | bytes 884744 | tf_op jit(solution)/shard_map/ppermute | solution.py:253
  87.8 9.3 %collective-permute-start.6 = (bf16[8,32,576]{2,1,0:T(8,128)(2,1)S(1)}, bf16[8,32,576]{2,1,0:T(8,128)(2,1)}, u32[]{:S(2)}, u32[]{:S(2)}) collective-permute-start(bf16[8,32,576]{2,1,0:T(8,128)(2,1)S(1)} %get-tuple-element.49), channel_id=1, source_target_pairs={{0,3},{1,0},{2,1},{3,2},{4,7},{5,4},{6,5},{7,6},{8,11},{9,8},{10,9... | collective-permute-start | bytes 884744 | tf_op jit(solution)/shard_map/ppermute | solution.py:253
  91.7 14.1 %collective-permute-start.16 = (bf16[128,1024]{1,0:T(8,128)(2,1)S(1)}, bf16[128,1024]{1,0:T(8,128)(2,1)}, u32[]{:S(2)}, u32[]{:S(2)}) collective-permute-start(bf16[128,1024]{1,0:T(8,128)(2,1)S(1)} %collective-permute-done.14.refs_1_), channel_id=1, source_target_pairs={{0,16},{4,20},{16,24},{20,28},{24,8},{28,12},{8,0},{12,4},{1,17},{... | collective-permute-start | bytes 786440 | tf_op jit(solution)/shard_map/ppermute | solution.py:51
  92.6 13.2 %collective-permute-start.18 = (bf16[128,1024]{1,0:T(8,128)(2,1)S(1)}, bf16[128,1024]{1,0:T(8,128)(2,1)S(1)}, u32[]{:S(2)}, u32[]{:S(2)}) collective-permute-start(bf16[128,1024]{1,0:T(8,128)(2,1)S(1)} %collective-permute-done.14.refs_1_), channel_id=1, source_target_pairs={{0,4},{4,0},{8,12},{12,8},{16,20},{20,16},{24,28},{28,24},{1,5},{5... | collective-permute-start | bytes 786440 | tf_op jit(solution)/shard_map/ppermute | solution.py:61
  95.9 11.3 %collective-permute-start.19 = (bf16[128,1024]{1,0:T(8,128)(2,1)S(1)}, bf16[128,1024]{1,0:T(8,128)(2,1)S(1)}, u32[]{:S(2)}, u32[]{:S(2)}) collective-permute-start(bf16[128,1024]{1,0:T(8,128)(2,1)S(1)} %collective-permute-done.15.refs_2_), channel_id=1, source_target_pairs={{0,4},{4,0},{8,12},{12,8},{16,20},{20,16},{24,28},{28,24},{1,5},{5... | collective-permute-start | bytes 786440 | tf_op jit(solution)/shard_map/ppermute | solution.py:61
  97.1 13.7 %collective-permute-start.9 = (bf16[128,1024]{1,0:T(8,128)(2,1)}, bf16[128,1024]{1,0:T(8,128)(2,1)S(1)}, u32[]{:S(2)}, u32[]{:S(2)}) collective-permute-start(bf16[128,1024]{1,0:T(8,128)(2,1)} %collective-permute-done.7.refs_1_), channel_id=1, source_target_pairs={{0,16},{4,20},{16,24},{20,28},{24,8},{28,12},{8,0},{12,4},{1,17},{... | collective-permute-start | bytes 786440 | tf_op jit(solution)/shard_map/ppermute | solution.py:51
  105.9 9.5 %collective-permute-start.25 = (bf16[128,1536]{1,0:T(8,128)(2,1)}, bf16[128,1536]{1,0:T(8,128)(2,1)}, u32[]{:S(2)}, u32[]{:S(2)}) collective-permute-start(bf16[128,1536]{1,0:T(8,128)(2,1)} %collective-permute-done.21.refs_1_), channel_id=1, source_target_pairs={{0,4},{4,0},{8,12},{12,8},{16,20},{20,16},{24,28},{28,24},{1,5},{5... | collective-permute-start | bytes 1179656 | tf_op jit(solution)/shard_map/ppermute | solution.py:61
  105.9 9.5 %collective-permute-start.26 = (bf16[128,1536]{1,0:T(8,128)(2,1)}, bf16[128,1536]{1,0:T(8,128)(2,1)}, u32[]{:S(2)}, u32[]{:S(2)}) collective-permute-start(bf16[128,1536]{1,0:T(8,128)(2,1)} %collective-permute-done.22.refs_2_), channel_id=1, source_target_pairs={{0,4},{4,0},{8,12},{12,8},{16,20},{20,16},{24,28},{28,24},{1,5},{5... | collective-permute-start | bytes 1179656 | tf_op jit(solution)/shard_map/ppermute | solution.py:61
  106.4 9.5 %collective-permute-start.27 = (bf16[128,1536]{1,0:T(8,128)(2,1)}, bf16[128,1536]{1,0:T(8,128)(2,1)}, u32[]{:S(2)}, u32[]{:S(2)}) collective-permute-start(bf16[128,1536]{1,0:T(8,128)(2,1)} %collective-permute-done.23.refs_3_), channel_id=1, source_target_pairs={{0,4},{4,0},{8,12},{12,8},{16,20},{20,16},{24,28},{28,24},{1,5},{5... | collective-permute-start | bytes 1179656 | tf_op jit(solution)/shard_map/ppermute | solution.py:61
  107.2 20.3 %collective-permute-start.11 = (bf16[128,1024]{1,0:T(8,128)(2,1)}, bf16[128,1024]{1,0:T(8,128)(2,1)}, u32[]{:S(2)}, u32[]{:S(2)}) collective-permute-start(bf16[128,1024]{1,0:T(8,128)(2,1)} %collective-permute-done.7.refs_1_), channel_id=1, source_target_pairs={{0,4},{4,0},{8,12},{12,8},{16,20},{20,16},{24,28},{28,24},{1,5},{5... | collective-permute-start | bytes 786440 | tf_op jit(solution)/shard_map/ppermute | solution.py:61
  110.9 17.2 %collective-permute-start.20 = (bf16[128,1024]{1,0:T(8,128)(2,1)}, bf16[128,1024]{1,0:T(8,128)(2,1)}, u32[]{:S(2)}, u32[]{:S(2)}) collective-permute-start(bf16[128,1024]{1,0:T(8,128)(2,1)} %collective-permute-done.16.refs_3_), channel_id=1, source_target_pairs={{0,4},{4,0},{8,12},{12,8},{16,20},{20,16},{24,28},{28,24},{1,5},{5... | collective-permute-start | bytes 786440 | tf_op jit(solution)/shard_map/ppermute | solution.py:61
  115.4 21.7 %collective-permute-start.12 = (bf16[128,1024]{1,0:T(8,128)(2,1)S(1)}, bf16[128,1024]{1,0:T(8,128)(2,1)S(1)}, u32[]{:S(2)}, u32[]{:S(2)}) collective-permute-start(bf16[128,1024]{1,0:T(8,128)(2,1)S(1)} %copy-done.13), channel_id=1, source_target_pairs={{0,4},{4,0},{8,12},{12,8},{16,20},{20,16},{24,28},{28,24},{1,5},{5... | collective-permute-start | bytes 786440 | tf_op jit(solution)/shard_map/ppermute | solution.py:61
  115.4 31.9 %collective-permute-start.34 = (bf16[32,3584]{1,0:T(8,128)(2,1)S(1)}, bf16[32,3584]{1,0:T(8,128)(2,1)S(1)}, u32[]{:S(2)}, u32[]{:S(2)}) collective-permute-start(bf16[32,3584]{1,0:T(8,128)(2,1)S(1)} %copy-done.32), channel_id=1, source_target_pairs={{0,4},{4,0},{8,12},{12,8},{16,20},{20,16},{24,28},{28,24},{1,5},{5... | collective-permute-start | bytes 688136 | tf_op jit(solution)/shard_map/ppermute | solution.py:61
  115.9 21.7 %collective-permute-start.13 = (bf16[128,1024]{1,0:T(8,128)(2,1)S(1)}, bf16[128,1024]{1,0:T(8,128)(2,1)S(1)}, u32[]{:S(2)}, u32[]{:S(2)}) collective-permute-start(bf16[128,1024]{1,0:T(8,128)(2,1)S(1)} %copy-done.17), channel_id=1, source_target_pairs={{0,4},{4,0},{8,12},{12,8},{16,20},{20,16},{24,28},{28,24},{1,5},{5... | collective-permute-start | bytes 786440 | tf_op jit(solution)/shard_map/ppermute | solution.py:61
  127.5 28.7 %collective-permute-start.43 = (bf16[32,3584]{1,0:T(8,128)(2,1)S(1)}, bf16[32,3584]{1,0:T(8,128)(2,1)S(1)}, u32[]{:S(2)}, u32[]{:S(2)}) collective-permute-start(bf16[32,3584]{1,0:T(8,128)(2,1)S(1)} %bitcast.99), channel_id=1, source_target_pairs={{0,4},{4,0},{8,12},{12,8},{16,20},{20,16},{24,28},{28,24},{1,5},{5... | collective-permute-start | bytes 688136 | tf_op jit(solution)/shard_map/ppermute | solution.py:61
  128.0 29.7 %collective-permute-start.44 = (bf16[32,3584]{1,0:T(8,128)(2,1)S(1)}, bf16[32,3584]{1,0:T(8,128)(2,1)S(1)}, u32[]{:S(2)}, u32[]{:S(2)}) collective-permute-start(bf16[32,3584]{1,0:T(8,128)(2,1)S(1)} %copy-done.23), channel_id=1, source_target_pairs={{0,4},{4,0},{8,12},{12,8},{16,20},{20,16},{24,28},{28,24},{1,5},{5... | collective-permute-start | bytes 688136 | tf_op jit(solution)/shard_map/ppermute | solution.py:61
  137.1 20.9 %collective-permute-start.45 = (bf16[32,3584]{1,0:T(8,128)(2,1)S(1)}, bf16[32,3584]{1,0:T(8,128)(2,1)S(1)}, u32[]{:S(2)}, u32[]{:S(2)}) collective-permute-start(bf16[32,3584]{1,0:T(8,128)(2,1)S(1)} %copy-done.28), channel_id=1, source_target_pairs={{0,4},{4,0},{8,12},{12,8},{16,20},{20,16},{24,28},{28,24},{1,5},{5... | collective-permute-start | bytes 688136 | tf_op jit(solution)/shard_map/ppermute | solution.py:61
  137.6 20.4 %collective-permute-start.46 = (bf16[32,3584]{1,0:T(8,128)(2,1)S(1)}, bf16[32,3584]{1,0:T(8,128)(2,1)S(1)}, u32[]{:S(2)}, u32[]{:S(2)}) collective-permute-start(bf16[32,3584]{1,0:T(8,128)(2,1)S(1)} %copy-done.30), channel_id=1, source_target_pairs={{0,4},{4,0},{8,12},{12,8},{16,20},{20,16},{24,28},{28,24},{1,5},{5... | collective-permute-start | bytes 688136 | tf_op jit(solution)/shard_map/ppermute | solution.py:61
  153.5 13.8 %collective-permute-start.35 = (f32[2,32,576]{2,1,0:T(8,128)}, f32[2,32,576]{2,1,0:T(8,128)S(1)}, u32[]{:S(2)}, u32[]{:S(2)}) collective-permute-start(f32[2,32,576]{2,1,0:T(8,128)} %get-tuple-element.37), channel_id=1, source_target_pairs={{0,1},{1,2},{2,3},{3,0},{4,5},{5,6},{6,7},{7,4},{8,9},{9,10},{10,1... | collective-permute-start | bytes 442376 | tf_op jit(solution)/shard_map/ppermute | solution.py:273
  156.3 13.0 %collective-permute-start.36 = (f32[2,32,576]{2,1,0:T(8,128)}, f32[2,32,576]{2,1,0:T(8,128)S(1)}, u32[]{:S(2)}, u32[]{:S(2)}) collective-permute-start(f32[2,32,576]{2,1,0:T(8,128)} %get-tuple-element.38), channel_id=1, source_target_pairs={{0,2},{1,3},{2,0},{3,1},{4,6},{5,7},{6,4},{7,5},{8,10},{9,11},{10,... | collective-permute-start | bytes 442376 | tf_op jit(solution)/shard_map/ppermute | solution.py:273
  157.8 11.5 %collective-permute-start.37 = (f32[2,32,576]{2,1,0:T(8,128)}, f32[2,32,576]{2,1,0:T(8,128)S(1)}, u32[]{:S(2)}, u32[]{:S(2)}) collective-permute-start(f32[2,32,576]{2,1,0:T(8,128)} %get-tuple-element.39), channel_id=1, source_target_pairs={{0,3},{1,0},{2,1},{3,2},{4,7},{5,4},{6,5},{7,6},{8,11},{9,8},{10,9... | collective-permute-start | bytes 442376 | tf_op jit(solution)/shard_map/ppermute | solution.py:273
  165.0 8.2 %collective-permute-start.47 = (f32[2,32,576]{2,1,0:T(8,128)}, f32[2,32,576]{2,1,0:T(8,128)S(1)}, u32[]{:S(2)}, u32[]{:S(2)}) collective-permute-start(f32[2,32,576]{2,1,0:T(8,128)} %get-tuple-element.41), channel_id=1, source_target_pairs={{0,1},{1,2},{2,3},{3,0},{4,5},{5,6},{6,7},{7,4},{8,9},{9,10},{10,1... | collective-permute-start | bytes 442376 | tf_op jit(solution)/shard_map/ppermute | solution.py:273
  166.8 8.3 %collective-permute-start.48 = (f32[2,32,576]{2,1,0:T(8,128)}, f32[2,32,576]{2,1,0:T(8,128)S(1)}, u32[]{:S(2)}, u32[]{:S(2)}) collective-permute-start(f32[2,32,576]{2,1,0:T(8,128)} %get-tuple-element.42), channel_id=1, source_target_pairs={{0,2},{1,3},{2,0},{3,1},{4,6},{5,7},{6,4},{7,5},{8,10},{9,11},{10,... | collective-permute-start | bytes 442376 | tf_op jit(solution)/shard_map/ppermute | solution.py:273
  167.3 8.8 %collective-permute-start.49 = (f32[2,32,576]{2,1,0:T(8,128)}, f32[2,32,576]{2,1,0:T(8,128)S(1)}, u32[]{:S(2)}, u32[]{:S(2)}) collective-permute-start(f32[2,32,576]{2,1,0:T(8,128)} %get-tuple-element.43), channel_id=1, source_target_pairs={{0,3},{1,0},{2,1},{3,2},{4,7},{5,4},{6,5},{7,6},{8,11},{9,8},{10,9... | collective-permute-start | bytes 442376 | tf_op jit(solution)/shard_map/ppermute | solution.py:273
  169.4 8.5 %collective-permute-start.38 = (bf16[32,576]{1,0:T(8,128)(2,1)S(1)}, bf16[32,576]{1,0:T(8,128)(2,1)S(1)}, u32[]{:S(2)}, u32[]{:S(2)}) collective-permute-start(bf16[32,576]{1,0:T(8,128)(2,1)S(1)} %get-tuple-element.58), channel_id=1, source_target_pairs={{0,4},{1,12},{2,20},{3,28},{4,0},{5,8},{6,16},{7,24},{8,5},{9,13},... | collective-permute-start | bytes 110600 | tf_op jit(solution)/shard_map/ppermute | solution.py:285
  169.4 8.4 %collective-permute-start.39 = (bf16[32,576]{1,0:T(8,128)(2,1)S(1)}, bf16[32,576]{1,0:T(8,128)(2,1)S(1)}, u32[]{:S(2)}, u32[]{:S(2)}) collective-permute-start(bf16[32,576]{1,0:T(8,128)(2,1)S(1)} %get-tuple-element.59), channel_id=1, source_target_pairs={{0,0},{1,8},{2,16},{3,24},{4,4},{5,12},{6,20},{7,28},{8,1},{9,9},{... | collective-permute-start | bytes 110600 | tf_op jit(solution)/shard_map/ppermute | solution.py:285
  177.1 1.3 collective-permute-start.50
  177.2 1.2 collective-permute-start.51
  178.6 8.8 %collective-permute-start.52 = (f32[64,1]{0,1:T(1,128)S(1)}, f32[64,1]{0,1:T(1,128)S(1)}, u32[]{:S(2)}, u32[]{:S(2)}) collective-permute-start(f32[64,1]{0,1:T(1,128)S(1)} %bitcast.111), channel_id=1, source_target_pairs={{0,1},{1,0},{2,3},{3,2},{4,5},{5,4},{6,7},{7,6},{8,9},{9,8},{10,11... | collective-permute-start | bytes 776 | tf_op jit(solution)/shard_map/ppermute | solution.py:181
  187.5 7.4 %collective-permute-start.53 = (f32[64,1]{0,1:T(1,128)S(1)}, f32[64,1]{0,1:T(1,128)S(1)}, u32[]{:S(2)}, u32[]{:S(2)}) collective-permute-start(f32[64,1]{0,1:T(1,128)S(1)} %bitcast_add_fusion), channel_id=1, source_target_pairs={{0,2},{1,3},{2,0},{3,1},{4,6},{5,7},{6,4},{7,5},{8,10},{9,11},{10,... | collective-permute-start | bytes 776 | tf_op jit(solution)/shard_map/ppermute | solution.py:181
  (33 other events, 263.7 us)
